TPU v7x, 32 devices: a 4x4x1 block of a 4x4x8 slice. The times are simulated.
32 devices in a mesh: data: 1 (over z), seq: 4 (over y), dap: 8 (over x, core).
Axes of the slice: x: 4, y: 4, z: 1, core: 2. Of those that a mesh axis runs over, the one named last changes fastest.
The devices are a block of a 4x4x8 slice.
Arguments:
- msa_act: bfloat16 [2048, 256, 64], P(('data', 'seq'), 'dap')
- msa_mask: int32 [2048, 256], P('data')
- pair_act: float32 [256, 256, 128], P(('data', 'dap'))
- ln_gamma: bfloat16 [64], replicated
- ln_beta: bfloat16 [64], replicated
- w_left: bfloat16 [64, 32], replicated
- b_left: bfloat16 [32], replicated
- w_right: bfloat16 [64, 32], replicated
- b_right: bfloat16 [32], replicated
- w_out: bfloat16 [1024, 128], replicated
- b_out: bfloat16 [128], replicated
Outputs:
- output 1: float32 [256, 256, 128], P(('data', 'dap'))
- output 2: bfloat16 [2048, 256, 64], P(('data', 'seq', 'dap'))
All inputs are finite; a program needn't handle non-finite values.
Results may differ from a plain program's by a relative error of at most 0.0120149.
Values are sent between devices in bfloat16 or wider.
A program may use at most 768 MiB of HBM per device.

v0:
```python
import jax
import jax.numpy as jnp
from jax import lax
from jax.sharding import PartitionSpec as P


def block_rows(rows_total, row_width):
    target = max(1, 16384 // row_width)
    return max(divisor for divisor in range(1, min(rows_total, target) + 1) if rows_total % divisor == 0)


def layer_norm(value_a7, ln_gamma, ln_beta):
    act_f32 = value_a7.astype(jnp.float32)
    mean_val = jnp.mean(act_f32, axis=-1, keepdims=True)
    centered = act_f32 - mean_val
    var_val = jnp.mean(centered * centered, axis=-1, keepdims=True)
    normed = centered * lax.rsqrt(var_val + 1e-5)
    return (normed * ln_gamma.astype(jnp.float32) + ln_beta.astype(jnp.float32)).astype(jnp.bfloat16)


def project(normed, weight, bias_vec, mask_f32):
    flat_act = normed.reshape(-1, normed.shape[-1])
    out_f32 = jnp.dot(flat_act, weight, preferred_element_type=jnp.float32) + bias_vec.astype(jnp.float32)
    return (out_f32.reshape(normed.shape[:-1] + (weight.shape[1],)) * mask_f32[:, :, None]).astype(jnp.bfloat16)


def pair_partial(left_proj, right_proj, w_out3):
    n_seq = left_proj.shape[0]
    n_rows = left_proj.shape[1]
    c_hid = left_proj.shape[2]
    n_cols = right_proj.shape[1]
    rows_per = block_rows(n_rows, n_cols)
    left_blocks = jnp.moveaxis(left_proj.reshape(n_seq, n_rows // rows_per, rows_per, c_hid), 1, 0)

    def one_block(left_blk):
        outer_blk = jnp.einsum('sic,sjd->icjd', left_blk, right_proj, preferred_element_type=jnp.float32).astype(jnp.bfloat16)
        return jnp.einsum('icjd,cde->ije', outer_blk, w_out3, preferred_element_type=jnp.float32).astype(jnp.bfloat16)

    return lax.map(one_block, left_blocks).reshape(n_rows, n_cols, w_out3.shape[2])


def solution(mesh):
    dap_size = mesh.shape['dap']
    replicated = P()
    in_specs = (P(('data', 'seq'), 'dap', None), P('data', None), P(('data', 'dap'), None, None), replicated, replicated, replicated, replicated, replicated, replicated, replicated, replicated)
    out_specs = (P(('data', 'dap'), None, None), P(('data', 'seq', 'dap'), None, None))

    def local_fn(array_b7, mask_part, pair_rows, ln_gamma, ln_beta, w_left, b_left, w_right, b_right, w_out, b_out):
        seq_idx = lax.axis_index('seq')
        dap_idx = lax.axis_index('dap')
        local_c7 = lax.all_to_all(array_b7, 'dap', 0, 1, tiled=True)
        n_local = local_c7.shape[0]
        n_rows = pair_rows.shape[0]
        c_hid = w_left.shape[1]
        mask_seq = lax.dynamic_slice_in_dim(mask_part, (seq_idx * dap_size + dap_idx) * n_local, n_local, axis=0).astype(jnp.float32)
        normed = layer_norm(local_c7, ln_gamma, ln_beta)
        left_proj = project(normed, w_left, b_left, mask_seq)
        right_proj = project(normed, w_right, b_right, mask_seq)
        w_out3 = w_out.reshape(c_hid, c_hid, w_out.shape[1])
        partial = pair_partial(left_proj, right_proj, w_out3)
        summed = lax.psum_scatter(partial, 'dap', scatter_dimension=0, tiled=True)
        summed = lax.psum(summed, 'seq')
        mask_bf16 = mask_part.astype(jnp.bfloat16)
        mask_rows = lax.dynamic_slice_in_dim(mask_bf16, dap_idx * n_rows, n_rows, axis=1)
        pair_count = jnp.einsum('si,sj->ij', mask_rows, mask_bf16, preferred_element_type=jnp.float32)
        update = (summed.astype(jnp.float32) + b_out.astype(jnp.float32)) / (1e-3 + pair_count)[:, :, None]
        return pair_rows + update, local_c7

    return jax.shard_map(local_fn, mesh=mesh, in_specs=in_specs, out_specs=out_specs, check_vma=False)
```

profile of v0, /device:TPU:97, one launch (start us, length us, event | category | flops | bytes accessed | tf_op | source)
XLA Modules:
  0.0 343.6 jit_solution(13179219632723588693)
XLA Ops:
  7.2 0.0 copy-start
  7.2 7.4 %copy.23 = bf16[512,32,64]{2,1,0:T(8,128)(2,1)} copy(bf16[512,32,64]{0,2,1:T(8,128)(2,1)} %param.13) | data formatting | bytes 4194304 | tf_op args[0]
  14.6 0.0 copy-start.5
  14.6 0.0 copy-start.6
  14.6 0.0 copy-start.7
  14.6 0.0 copy-start.8
  14.6 7.6 %reshape.74 = bf16[8,2,65536]{2,1,0:T(2,128)(2,1)} reshape(bf16[512,32,64]{2,1,0:T(8,128)(2,1)} %copy.23) | data formatting | bytes 4194304
  22.2 6.0 %all-to-all-start = ((bf16[8,2,65536]{2,1,0:T(2,128)(2,1)}), bf16[8,2,65536]{2,1,0:T(2,128)(2,1)S(1)}, u32[]{:S(2)}, u32[]{:S(2)}) async-start(bf16[8,2,65536]{2,1,0:T(2,128)(2,1)} %reshape.74), calls=%async_computation | async-start | bytes 4194304 | tf_op jit(solution)/shard_map/all_to_all | solution.py:51
  28.2 0.0 reduce-scatter.2.cloned.1.call-start
  28.2 0.0 copy-done.5
  28.3 0.0 copy-done.6
  28.3 0.0 copy-done.7
  28.3 0.0 copy-done.8
  28.3 0.9 dynamic-slice_convert_fusion
  29.2 0.1 copy.32
  29.3 25.0 %all-to-all-done = bf16[8,2,65536]{2,1,0:T(2,128)(2,1)S(1)} async-done(((bf16[8,2,65536]{2,1,0:T(2,128)(2,1)}), bf16[8,2,65536]{2,1,0:T(2,128)(2,1)S(1)}, u32[]{:S(2)}, u32[]{:S(2)}) %all-to-all-start) | async-done | bytes 2097184 | tf_op jit(solution)/shard_map/all_to_all | solution.py:51
  54.2 4.9 %reshape.75 = bf16[512,32,64]{2,1,0:T(8,128)(2,1)} reshape(bf16[8,2,65536]{2,1,0:T(2,128)(2,1)S(1)} %all-to-all-done) | data formatting | bytes 4194304
  59.2 4.4 %fusion.21 = f32[64,8,32]{2,1,0:T(8,128)S(1)} fusion(bf16[8,64,32,64]{3,2,1,0:T(8,128)(2,1)} %bitcast.73), kind=kLoop, calls=%fused_computation.20 | loop fusion | flops 2080768 | bytes 2162688 | tf_op jit(solution)/shard_map/reduce_sum | solution.py:14
  63.6 0.1 div.17
  63.8 0.0 copy-start.2
  63.8 6.2 %multiply_reduce_fusion = f32[64,8,32]{2,1,0:T(8,128)S(1)} fusion(f32[64,8,32]{2,1,0:T(8,128)S(1)} %broadcast_multiply_fusion, bf16[8,64,32,64]{3,2,1,0:T(8,128)(2,1)} %bitcast.74), kind=kLoop, calls=%fused_computation.18 | loop fusion | flops 4177920 | bytes 2228224 | tf_op jit(solution)/shard_map/reduce_sum | solution.py:16
  70.0 0.0 copy-done.2
  70.0 6.2 %fusion.26 = (bf16[8,64,32,64]{3,2,0,1:T(8,128)(2,1)}, f32[64,8,32,64]{3,2,1,0:T(8,128)}) fusion(bf16[512,32,64]{2,1,0:T(8,128)(2,1)S(1)} %copy-done.2), kind=kLoop, calls=%fused_computation.32 | loop fusion | flops 1048576 | bytes 8388608 | tf_op jit(solution)/shard_map/all_to_all | solution.py:51
  76.2 0.1 rsqrt.12
  76.3 12.2 %fusion.20 = bf16[16384,64]{1,0:T(8,128)(2,1)S(1)} fusion(f32[64,8,32,64]{3,2,1,0:T(8,128)} %get-tuple-element.45, f32[64]{0:T(128)S(1)} %convert_element_type.56, f32[64]{0:T(128)S(1)} %convert_element_type.55, f32[16384]{0:T(1024)S(1)} %rsqrt.12, f32[16384]{0:T(1024)S(1)} %div.17), kind=kLoop, calls=%fused_computation.17 | loop fusion | flops 5242880 | bytes 6423040 | tf_op jit(solution)/shard_map/convert_element_type | solution.py:18
  88.5 0.0 copy-done
  88.5 1.5 convolution_add_fusion
  90.1 0.0 copy-start.4
  90.1 0.6 copy.33
  90.7 0.3 fusion.23
  91.0 0.0 copy-done.4
  91.0 1.5 convolution_add_fusion.1
  92.5 4.2 %reshape.65 = f32[64,4,64,32]{2,1,0,3:T(4,128)} reshape(f32[16384,32]{0,1:T(8,128)S(1)} %convolution_add_fusion.1) | data formatting | bytes 4194304 | tf_op jit(solution)/shard_map/reshape | solution.py:24
  96.7 5.3 %copy.26 = f32[64,4,64,32]{0,3,2,1:T(8,128)} copy(f32[64,4,64,32]{2,1,0,3:T(4,128)} %reshape.65) | data formatting | bytes 4194304 | tf_op jit(solution)/shard_map/reshape | solution.py:24
  102.1 2.9 fusion.22
  105.0 80.7 %while.10 = (s32[]{:T(128)}, bf16[4,64,256,128]{3,2,1,0:T(8,128)(2,1)}, bf16[4,64,64,32]{1,3,2,0:T(8,128)(2,1)S(1)}, bf16[64,256,32]{1,0,2:T(8,128)(2,1)S(1)}, bf16[32,32,128]{2,1,0:T(8,128)(2,1)}, /*index=5*/s32[]{:T(128)}) while((s32[]{:T(128)}, bf16[4,64,256,128]{3,2,1,0:T(8,128)(2,1)}, bf16[4,64,64,32]{1,3,2,0:T(8,128)(2,1)S(1)}, ...), condition=%wide.region_3.4_spmd, body=%wide.region_2.3_spmd.sunk | while | flops 6461325312 | bytes 6030413 | solution.py:39
  105.2 20.1 %fusion.42 = bf16[4,64,256,128]{3,2,1,0:T(8,128)(2,1)} fusion(bf16[4,64,256,128]{3,2,1,0:T(8,128)(2,1)} %get-tuple-element.84, s32[]{:T(128)S(6)} %copy.45, bf16[64,256,32]{1,0,2:T(8,128)(2,1)S(1)} %get-tuple-element.92, bf16[4,64,64,32]{1,3,2,0:T(8,128)(2,1)S(1)} %get-tuple-element.91, bf16[32,32,128,1]{2,1,0,3:T(8,128)(2,1)} %bitcast.80), kind=kOutput, calls=%fused_computation.5.clone.1 | convolution fusion | flops 6461325312 | bytes 6030336 | tf_op jit(solution)/shard_map/while/body/eval_jaxpr/icjd,cde->ije/dot_general | solution.py:37
  125.3 20.1 %fusion.42 = bf16[4,64,256,128]{3,2,1,0:T(8,128)(2,1)} fusion(bf16[4,64,256,128]{3,2,1,0:T(8,128)(2,1)} %get-tuple-element.84, s32[]{:T(128)S(6)} %copy.45, bf16[64,256,32]{1,0,2:T(8,128)(2,1)S(1)} %get-tuple-element.92, bf16[4,64,64,32]{1,3,2,0:T(8,128)(2,1)S(1)} %get-tuple-element.91, bf16[32,32,128,1]{2,1,0,3:T(8,128)(2,1)} %bitcast.80), kind=kOutput, calls=%fused_computation.5.clone.1 | convolution fusion | flops 6461325312 | bytes 6030336 | tf_op jit(solution)/shard_map/while/body/eval_jaxpr/icjd,cde->ije/dot_general | solution.py:37
  145.5 20.1 %fusion.42 = bf16[4,64,256,128]{3,2,1,0:T(8,128)(2,1)} fusion(bf16[4,64,256,128]{3,2,1,0:T(8,128)(2,1)} %get-tuple-element.84, s32[]{:T(128)S(6)} %copy.45, bf16[64,256,32]{1,0,2:T(8,128)(2,1)S(1)} %get-tuple-element.92, bf16[4,64,64,32]{1,3,2,0:T(8,128)(2,1)S(1)} %get-tuple-element.91, bf16[32,32,128,1]{2,1,0,3:T(8,128)(2,1)} %bitcast.80), kind=kOutput, calls=%fused_computation.5.clone.1 | convolution fusion | flops 6461325312 | bytes 6030336 | tf_op jit(solution)/shard_map/while/body/eval_jaxpr/icjd,cde->ije/dot_general | solution.py:37
  165.6 20.1 %fusion.42 = bf16[4,64,256,128]{3,2,1,0:T(8,128)(2,1)} fusion(bf16[4,64,256,128]{3,2,1,0:T(8,128)(2,1)} %get-tuple-element.84, s32[]{:T(128)S(6)} %copy.45, bf16[64,256,32]{1,0,2:T(8,128)(2,1)S(1)} %get-tuple-element.92, bf16[4,64,64,32]{1,3,2,0:T(8,128)(2,1)S(1)} %get-tuple-element.91, bf16[32,32,128,1]{2,1,0,3:T(8,128)(2,1)} %bitcast.80), kind=kOutput, calls=%fused_computation.5.clone.1 | convolution fusion | flops 6461325312 | bytes 6030336 | tf_op jit(solution)/shard_map/while/body/eval_jaxpr/icjd,cde->ije/dot_general | solution.py:37
  185.6 0.0 copy-start.3
  185.6 0.1 reduce-scatter.2.cloned.1.call-update
  185.7 0.0 copy-start.9
  185.7 0.1 all-reduce.2.cloned.1.call-start
  185.8 90.4 %reduce-scatter.2.cloned.1.call-done = bf16[32,256,128]{2,1,0:T(8,128)(2,1)} async-done(((bf16[256,256,128]{2,1,0:T(8,128)(2,1)}), bf16[32,256,128]{2,1,0:T(8,128)(2,1)}) %reduce-scatter.2.cloned.1.call-update) | async-done | bytes 2097168 | tf_op jit(solution)/shard_map/reduce_scatter | solution.py:61
  276.2 0.1 all-reduce.2.cloned.1.call-update
  276.3 0.0 copy-done.3
  276.3 0.2 convert_element_type.65
  276.5 0.0 copy-done.9
  276.6 0.5 convolution_add_fusion.2
  277.1 0.0 copy-start.1
  277.1 4.8 %copy.27 = bf16[64,256,64]{1,2,0:T(8,128)(2,1)} copy(bf16[64,256,64]{2,1,0:T(8,128)(2,1)} %bitcast.76) | data formatting | bytes 4194304
  281.9 50.1 %all-reduce.2.cloned.1.call-done = bf16[32,256,128]{2,1,0:T(8,128)(2,1)} async-done(((bf16[32,256,128]{2,1,0:T(8,128)(2,1)}), bf16[32,256,128]{2,1,0:T(8,128)(2,1)}) %all-reduce.2.cloned.1.call-update) | async-done | bytes 2097168 | tf_op jit(solution)/shard_map/psum | solution.py:62
  332.0 4.7 %divide_add_fusion = f32[32,256,128]{2,1,0:T(8,128)} fusion(f32[32,256,128]{2,1,0:T(8,128)} %param.15, bf16[32,256,128]{2,1,0:T(8,128)(2,1)} %all-reduce.2.cloned.1.call-done, f32[32,256]{1,0:T(8,128)S(1)} %convolution_add_fusion.2, f32[128]{0:T(128)S(1)} %convert_element_type.64), kind=kLoop, calls=%fused_computation.21 | loop fusion | flops 4194304 | bytes 10519040 | tf_op jit(solution)/shard_map/add | solution.py:67
  336.7 0.0 copy-done.1
  (8 shorter events, 0.1 us)
Async XLA Ops:
  7.2 81.3 %copy-start = (bf16[64,32]{0,1:T(8,128)(2,1)S(1)}, bf16[64,32]{0,1:T(8,128)(2,1)}, u32[]{:S(2)}) copy-start(bf16[64,32]{0,1:T(8,128)(2,1)} %param.20) | copy-start | bytes 12292
  14.6 13.6 %copy-start.5 = (bf16[64]{0:T(256)(128)(2,1)S(1)}, bf16[64]{0:T(256)(128)(2,1)}, u32[]{:S(2)}) copy-start(bf16[64]{0:T(256)(128)(2,1)} %param.16) | copy-start | bytes 388
  14.6 13.7 %copy-start.6 = (bf16[64]{0:T(256)(128)(2,1)S(1)}, bf16[64]{0:T(256)(128)(2,1)}, u32[]{:S(2)}) copy-start(bf16[64]{0:T(256)(128)(2,1)} %param.17) | copy-start | bytes 388
  14.6 13.7 %copy-start.7 = (bf16[32]{0:T(256)(128)(2,1)S(1)}, bf16[32]{0:T(256)(128)(2,1)}, u32[]{:S(2)}) copy-start(bf16[32]{0:T(256)(128)(2,1)} %param.19) | copy-start | bytes 196
  14.6 13.7 %copy-start.8 = (bf16[32]{0:T(256)(128)(2,1)S(1)}, bf16[32]{0:T(256)(128)(2,1)}, u32[]{:S(2)}) copy-start(bf16[32]{0:T(256)(128)(2,1)} %param.21) | copy-start | bytes 196
  22.2 32.0 %all-to-all-start = ((bf16[8,2,65536]{2,1,0:T(2,128)(2,1)}), bf16[8,2,65536]{2,1,0:T(2,128)(2,1)S(1)}, u32[]{:S(2)}, u32[]{:S(2)}) async-start(bf16[8,2,65536]{2,1,0:T(2,128)(2,1)} %reshape.74), calls=%async_computation | async-start | bytes 4194304 | tf_op jit(solution)/shard_map/all_to_all | solution.py:51
  28.2 248.0 %reduce-scatter.2.cloned.1.call-start = ((), (), s32[]{:S(2)}) async-start(), calls=%async_computation.2 | async-start | bytes 18874368 | tf_op jit(solution)/shard_map/reduce_scatter | solution.py:61
  63.8 6.2 %copy-start.2 = (bf16[512,32,64]{2,1,0:T(8,128)(2,1)S(1)}, bf16[512,32,64]{2,1,0:T(8,128)(2,1)}, u32[]{:S(2)}) copy-start(bf16[512,32,64]{2,1,0:T(8,128)(2,1)} %reshape.75) | copy-start | bytes 6291460
  90.1 0.9 copy-start.4
  185.6 90.7 %copy-start.3 = (s32[2048,256]{1,0:T(8,128)S(1)}, s32[2048,256]{1,0:T(8,128)}, u32[]{:S(2)}) copy-start(s32[2048,256]{1,0:T(8,128)} %param.14) | copy-start | bytes 6291460
  185.7 90.8 %copy-start.9 = (bf16[128]{0:T(256)(128)(2,1)S(1)}, bf16[128]{0:T(256)(128)(2,1)}, u32[]{:S(2)}) copy-start(bf16[128]{0:T(256)(128)(2,1)} %param.23) | copy-start | bytes 772
  185.7 146.3 %all-reduce.2.cloned.1.call-start = ((), (), s32[]{:S(2)}) async-start(), calls=%async_computation.3 | async-start | bytes 4194304 | tf_op jit(solution)/shard_map/psum | solution.py:62
  277.1 59.7 %copy-start.1 = (bf16[64,32]{0,1:T(8,128)(2,1)S(1)}, bf16[64,32]{0,1:T(8,128)(2,1)}, u32[]{:S(2)}) copy-start(bf16[64,32]{0,1:T(8,128)(2,1)} %param.20) | copy-start | bytes 12292
Sparse Core Ops, SparseCore 0:
  185.8 90.3 reduce-scatter.1
  278.6 53.3 all-reduce.1
where the time goes:
time: 345 us; the launch traced here: 344 us
  waiting for transfers between devices  166 us (48%)
  matrix products  84 us (24%)
  other arithmetic  38 us (11%)
  local copies, waits for them, and re-layouts  35.3 us (10%)
  between operations  14.3 us (4%)
  starting transfers between devices  6.08 us (2%)
    reduce_scatter x1, waiting for transfers between devices, local_fn(): summed = lax.psum_scatter(partial, 'dap', scatter_dimension=0, tiled=True)  90.4 us
    dot_general x4, matrix products, one_block(): jnp.einsum('icjd,cde->ije', outer_blk, w_out3, preferred_element_type=jnp...  80.4 us
    psum x1, waiting for transfers between devices, local_fn(): summed = lax.psum(summed, 'seq')  50.1 us
    unnamed x25, local copies, waits for them, and re-layouts  25.4 us
    all_to_all x1, waiting for transfers between devices, local_fn(): local_c7 = lax.all_to_all(array_b7, 'dap', 0, 1, tiled=True)  25 us
    convert_element_type x1, other arithmetic, layer_norm(): (normed * ln_gamma.astype(jnp.float32) + ln_beta.astype(jnp.float32)).ast...  12.2 us
    reshape x2, local copies, waits for them, and re-layouts, project(): out_f32.reshape(normed.shape[:-1] + (weight.shape[1],))  9.54 us
  transfers between devices with their start and end apart: 3, of which 3 were waited for; matrix products, arithmetic and copies ran while one was open for 2% of the time, Pallas kernels for 0%

commit v1 on v0

v1 whole, which is shorter than its diff:
```python
import functools
import jax
import jax.numpy as jnp
from jax import lax
from jax.experimental import pallas as pl
from jax.experimental.pallas import tpu as pltpu
from jax.sharding import PartitionSpec as P

F32 = jnp.float32
BF16 = jnp.bfloat16
LAG1 = 1
LAG2 = 2


def iota(shape, dim):
    return lax.broadcasted_iota(jnp.int32, shape, dim)


def onehot(cond):
    return jnp.where(cond, 1.0, 0.0).astype(BF16)


def dot(a, b):
    return jnp.dot(a, b, preferred_element_type=F32)


def dot_nt(a, b):
    return lax.dot_general(a, b, (((1,), (1,)), ((), ())), preferred_element_type=F32)


def dot_tn(a, b):
    return lax.dot_general(a, b, (((0,), (0,)), ((), ())), preferred_element_type=F32)


def kernel(dims, m_hbm, mask_hbm, z_hbm, vecs, waT, wbT, wo, zo_hbm, mo_hbm,
           mT, mkv, zv, xT, wbig, bbb, mkT, acat, bT, wblk, lbuf, rp, rq, sp, sq, rc, mr, tbuf, ov,
           sem_in, sem_out, bs_own, bs_fwd, bs_rel, b_recv, ms_dir, ms_opp, ms_fwd, ms_rel, m_recv, mf_recv, m_prel,
           y1s, y1r, y2s, y2r):
    n_y, n_d = dims
    n_x = n_d // 2
    yy = lax.axis_index("seq")
    dd = lax.axis_index("dap")
    xx = dd // 2
    cc = dd % 2
    x_r = (xx + 1) % n_x
    x_l = (xx + n_x - 1) % n_x
    x_o = (xx + 2) % n_x
    right, left, mate = 2 * x_r + cc, 2 * x_l + cc, 2 * xx + 1 - cc
    par = yy % 2
    y_a = yy + 1 - 2 * par
    y_b = (yy + n_y - 1 + 2 * par) % n_y
    n_i, n_ch, s_loc = mT.shape
    s_all, n_j = mkv.shape
    c_hid = waT.shape[0]
    half = n_i // 2
    hrows = half * c_hid
    s_chip = s_loc // n_x
    s_dev = s_loc // n_d

    def to_dap(idx):
        return dict(device_id={"dap": idx}, device_id_type=pl.DeviceIdType.MESH)

    def to_seq(idx):
        return dict(device_id={"seq": idx}, device_id_type=pl.DeviceIdType.MESH)

    in_m = pltpu.make_async_copy(m_hbm, mT, sem_in.at[0])
    in_mask = pltpu.make_async_copy(mask_hbm, mkv, sem_in.at[1])
    in_z = pltpu.make_async_copy(z_hbm, zv, sem_in.at[2])
    in_m.start()
    in_mask.start()
    in_z.start()

    barrier = pltpu.get_barrier_semaphore()
    for nb in (right, left, mate):
        pl.semaphore_signal(barrier, inc=1, **to_dap(nb))
    for nb in (y_a, y_b):
        pl.semaphore_signal(barrier, inc=1, **to_seq(nb))

    def remote(src, dst, ssem, rsem, to):
        return pltpu.make_async_remote_copy(src_ref=src, dst_ref=dst, send_sem=ssem, recv_sem=rsem, **to)

    def b_to(src_u, src_p, dst_u, dst_p, ssem, nb):
        return remote(bT.at[src_u, src_p], bT.at[dst_u, dst_p], ssem, b_recv.at[dst_u, dst_p], to_dap(nb))

    b_r0 = b_to(0, 0, 2, 0, bs_own.at[0], right)
    b_r1 = b_to(0, 1, 4, 0, bs_own.at[1], right)
    b_l1 = b_to(0, 1, 2, 1, bs_own.at[2], left)
    b_l0 = b_to(0, 0, 4, 1, bs_own.at[3], left)
    b_fr = b_to(2, 0, 6, 0, bs_fwd.at[0], right)
    b_fl = b_to(2, 1, 6, 1, bs_fwd.at[1], left)

    def b_rel(u, p):
        return b_to(u, p, u + 1, p, bs_rel.at[u, p], mate)

    def b_wait(u, p):
        b_to(u, p, u, p, bs_rel.at[u, p], mate).wait_recv()

    def lanes_of(xc):
        return pl.ds(pl.multiple_of(xc * s_chip, s_chip), s_chip)

    d_right, d_left, d_opp = 2 * x_r + cc, 2 * x_l + cc, 2 * x_o + cc
    up, lo = pl.ds(0, half), pl.ds(half, half)
    m_or = remote(mT.at[up, :, lanes_of(x_o)], tbuf.at[0], ms_opp.at[0], mf_recv.at[0], to_dap(right))
    m_ol = remote(mT.at[lo, :, lanes_of(x_o)], tbuf.at[1], ms_opp.at[1], mf_recv.at[1], to_dap(left))
    m_dr = remote(mT.at[:, :, lanes_of(x_r)], mr.at[dd], ms_dir.at[0], m_recv.at[0], to_dap(right))
    m_dl = remote(mT.at[:, :, lanes_of(x_l)], mr.at[dd], ms_dir.at[1], m_recv.at[1], to_dap(left))
    m_fr = remote(tbuf.at[0], mr.at[d_left, up], ms_fwd.at[0], m_recv.at[2], to_dap(right))
    m_fl = remote(tbuf.at[1], mr.at[d_right, lo], ms_fwd.at[1], m_recv.at[3], to_dap(left))
    m_p0 = remote(mT.at[:, :, lanes_of(xx)], mr.at[dd], ms_rel.at[0], m_prel.at[0], to_dap(mate))
    m_p1 = remote(mr.at[d_left], mr.at[d_left], ms_rel.at[1], m_prel.at[1], to_dap(mate))
    m_p2 = remote(mr.at[d_right], mr.at[d_right], ms_rel.at[2], m_prel.at[2], to_dap(mate))
    m_p3 = remote(mr.at[d_opp], mr.at[d_opp], ms_rel.at[3], m_prel.at[3], to_dap(mate))
    m_self = pltpu.make_async_copy(m_hbm.at[:, :, lanes_of(xx)], mr.at[dd], sem_in.at[3])

    def m_wait(ref, sem):
        remote(ref, ref, ms_rel.at[0], sem, to_dap(mate)).wait_recv()

    rowc = iota((hrows, c_hid), 0) // half
    rep_b = onehot(rowc == iota((hrows, c_hid), 1))
    gam, bet = vecs[0:1, 0:n_ch], vecs[1:2, 0:n_ch]
    ones_ch = jnp.ones((n_ch, 128), BF16)
    eye_ch = iota((n_ch, n_ch), 0) == iota((n_ch, n_ch), 1)
    gcol = dot(jnp.where(eye_ch, jnp.broadcast_to(gam, (n_ch, n_ch)), 0.0).astype(BF16), ones_ch)[:, 0:1]
    bcol = dot(jnp.where(eye_ch, jnp.broadcast_to(bet, (n_ch, n_ch)), 0.0).astype(BF16), ones_ch)[:, 0:1]
    eye_h = iota((c_hid, c_hid), 0) == iota((c_hid, c_hid), 1)
    bl = jnp.where(eye_h, jnp.broadcast_to(vecs[2:3, 0:c_hid], (c_hid, c_hid)), 0.0).astype(BF16)
    br = jnp.where(eye_h, jnp.broadcast_to(vecs[3:4, 0:c_hid], (c_hid, c_hid)), 0.0).astype(BF16)
    ones_h = jnp.ones((c_hid, 128), BF16)
    kb = half * n_ch
    tile_b = onehot(iota((n_ch, kb), 1) % n_ch == iota((n_ch, kb), 0))
    wrep = dot(rep_b, wbT[...]).astype(BF16)
    wide = dot(wrep, tile_b)
    keep = iota((hrows, kb), 0) % half == iota((hrows, kb), 1) // n_ch
    wbig[...] = jnp.where(keep, wide, 0.0).astype(BF16)
    brep = dot(dot(rep_b, br).astype(BF16), ones_h)[:, 0:n_i]
    bj = iota((hrows, n_i), 0) % half
    for h in range(2):
        bbb[h] = jnp.where(iota((hrows, n_i), 1) == bj + h * half, brep, 0.0).astype(BF16)

    in_mask.wait()
    selT = onehot(iota((n_i, n_j), 1) == iota((n_i, n_j), 0) + dd * n_i)
    mloc = mkv[pl.ds(pl.multiple_of(yy * s_loc, s_loc), s_loc), :].astype(F32).astype(BF16)
    mkT[...] = dot_nt(selT, mloc)

    in_m.wait()
    pl.semaphore_wait(barrier, 5)
    m_or.start()
    m_ol.start()
    m_p0.start()
    m_self.start()

    def norm_row(r, carry):
        act = mT[r].astype(F32)
        mean = jnp.sum(act, axis=0, keepdims=True) * (1.0 / n_ch)
        cen = act - mean
        var = jnp.sum(cen * cen, axis=0, keepdims=True) * (1.0 / n_ch)
        nrm = cen * lax.rsqrt(var + 1e-5)
        val = (nrm * gcol + bcol).astype(BF16).astype(F32) * mkT[pl.ds(r, 1), :]
        xT[pl.ds(pl.multiple_of(r * n_ch, n_ch), n_ch), :] = val.astype(BF16)
        return carry

    mk16 = mkT[...].astype(BF16)
    for h in range(2):
        lax.fori_loop(h * half, (h + 1) * half, norm_row, 0)
        for q in range(2):
            rows = slice(q * hrows // 2, (q + 1) * hrows // 2)
            acc = dot(wbig[rows, :], xT[h * kb:(h + 1) * kb, :]) + dot(bbb[h, rows, :], mk16)
            bT[0, h, rows, :] = acc.astype(BF16)
        if h == 0:
            b_r0.start()
        else:
            b_l1.start()
            b_l0.start()
            b_r1.start()
        b_rel(0, h).start()

    ga = 128 // c_hid
    ra = onehot(iota((128, c_hid), 0) % c_hid == iota((128, c_hid), 1))
    ka = ga * n_ch
    wa_rep = dot(dot(ra, waT[...]).astype(BF16), onehot(iota((n_ch, ka), 1) % n_ch == iota((n_ch, ka), 0)))
    wa4 = jnp.where(iota((128, ka), 0) // c_hid == iota((128, ka), 1) // n_ch, wa_rep, 0.0).astype(BF16)
    ba_rep = dot(dot(ra, bl).astype(BF16), ones_h)[:, 0:n_i]
    n_g = n_i // ga
    for g in range(n_g):
        bag = jnp.where(iota((128, n_i), 1) == iota((128, n_i), 0) // c_hid + ga * g, ba_rep, 0.0).astype(BF16)
        at = dot(wa4, xT[g * ka:(g + 1) * ka, :]) + dot(bag, mk16)
        acat[g // 2, :, (g % 2) * 128:(g % 2 + 1) * 128] = at.T.astype(BF16)

    n_e = wo.shape[1]
    wblk[...] = jnp.zeros_like(wblk)

    def place(dc, carry):
        r0, c0 = iota((128, c_hid * c_hid), 0), iota((128, c_hid * c_hid), 1)
        perm = onehot(c0 == (r0 % c_hid) * c_hid + dc * ga + r0 // c_hid)
        wp = dot(perm, wo[...]).astype(BF16)
        for k in range(ga):
            for i4 in range(ga):
                row = pl.multiple_of((dc * ga + k) * 128 + i4 * c_hid, c_hid)
                wblk[pl.ds(row, c_hid), i4 * n_e:(i4 + 1) * n_e] = wp[k * c_hid:(k + 1) * c_hid, :]
        return carry

    lax.fori_loop(0, c_hid // ga, place, 0)

    def pair_counts():
        sel = onehot(iota((n_j, 128), 0) == iota((n_j, 128), 1) + dd * n_i)
        rc[...] = jnp.zeros_like(rc)

        def add(k, carry):
            mk = mkv[pl.ds(pl.multiple_of(k * s_loc, s_loc), s_loc), :].astype(F32).astype(BF16)
            rc[...] += dot_tn(mk, dot(mk, sel).astype(BF16))
            return carry

        lax.fori_loop(0, s_all // s_loc, add, 0)
        rc[...] = 1.0 / (1e-3 + rc[...])

    def compute(t):
        def outer(q, carry):
            h, n = q // 4, q % 4
            acc = dot(bT[t, h], acat[n]).astype(BF16)
            for d in range(c_hid):
                for gg in range(2):
                    lbuf[(2 * n + gg) * 2 + h, :, d * 128:(d + 1) * 128] = acc[d * half:(d + 1) * half, gg * 128:(gg + 1) * 128]
            return carry

        lax.fori_loop(0, 8, outer, 0)
        for nn in range(2):
            cols = slice(nn * 256, (nn + 1) * 256)
            res = dot(lbuf[...].reshape(n_g * n_i, c_hid * 128), wblk[:, cols]).astype(BF16)
            for g in range(n_g):
                for k in range(2):
                    i = ga * g + 2 * nn + k
                    rp[t, i // half, i % half] = res[g * n_i:(g + 1) * n_i, k * 128:(k + 1) * 128]

    def y1(t, f):
        return remote(rp.at[t, f], rq.at[t, f], y1s.at[t, f], y1r.at[t, f], to_seq(y_a if f == 0 else y_b))

    def y2(t, f):
        return remote(sp.at[t, f], sq.at[t, f], y2s.at[t, f], y2r.at[t, f], to_seq(y_b if f == 0 else y_a))

    def j_of(t, p):
        u = t // 2
        off = jnp.where(u == 0, 0, jnp.where(u == 3, 2, n_x - 1 if p == 0 else 1))
        core = jnp.where(t % 2 == 0, cc, 1 - cc)
        hh = jnp.where(u == 2, 1 - p, p)
        return pl.multiple_of((2 * ((xx + off) % n_x) + core) * n_i + hh * half, half)

    def finish(t):
        for f in range(2):
            y2(t, f).wait_recv()
        for p in range(2):
            j0 = j_of(t, p)
            rcp = rc[pl.ds(j0, half), :]
            for i in range(n_i):
                rows = slice(p * half, (p + 1) * half)
                tot = sp[t, i // half, i % half, rows, :].astype(F32) + sq[t, i // half, i % half, rows, :].astype(F32)
                upd = (tot + vecs[4:5, :]) * jnp.broadcast_to(rcp[:, i:i + 1], (half, n_e))
                zv[i, pl.ds(j0, half), :] += upd

    def step(t, carry):
        @pl.when(t == 1)
        def _():
            b_wait(1, 0)
            b_wait(1, 1)

        @pl.when(t == 2)
        def _():
            b_wait(2, 0)
            b_fr.start()
            b_rel(2, 0).start()
            b_wait(2, 1)
            b_fl.start()
            b_rel(2, 1).start()
            m_wait(tbuf.at[0], mf_recv.at[0])
            m_fr.start()
            m_wait(tbuf.at[1], mf_recv.at[1])
            m_fl.start()
            m_dr.start()
            m_dl.start()

        @pl.when(t == 3)
        def _():
            b_wait(3, 0)
            b_wait(3, 1)

        @pl.when(t == 4)
        def _():
            b_wait(4, 0)
            b_rel(4, 0).start()
            b_wait(4, 1)
            b_rel(4, 1).start()

        @pl.when(t == 5)
        def _():
            b_wait(5, 0)
            b_wait(5, 1)

        @pl.when(t == 6)
        def _():
            b_wait(6, 0)
            b_rel(6, 0).start()
            b_wait(6, 1)
            b_rel(6, 1).start()

        @pl.when(t == 7)
        def _():
            b_wait(7, 0)
            b_wait(7, 1)

        @pl.when(t < 8)
        def _():
            compute(t)
            for f in range(2):
                y1(t, f).start()

        @pl.when(t == 1)
        def _():
            in_z.wait()
            pair_counts()

        @pl.when(jnp.logical_and(t >= LAG1, t < 8 + LAG1))
        def _():
            v = t - LAG1
            for f in range(2):
                y1(v, f).wait_recv()

                def add(i, carry):
                    tot = rp[v, f, i].astype(F32) + rq[v, f, i].astype(F32)
                    sp[v, f, i] = tot.astype(BF16)
                    return carry

                lax.fori_loop(0, half, add, 0)
                y2(v, f).start()

        @pl.when(t >= LAG2)
        def _():
            finish(t - LAG2)

        return carry

    lax.fori_loop(0, 8 + LAG2, step, 0)
    out_z = pltpu.make_async_copy(zv, zo_hbm, sem_out.at[0])
    out_z.start()

    m_wait(mr.at[d_opp, up], m_recv.at[2])
    m_wait(mr.at[d_opp, lo], m_recv.at[3])
    m_p3.start()
    m_wait(mr.at[d_left], m_recv.at[0])
    m_p1.start()
    m_wait(mr.at[d_right], m_recv.at[1])
    m_p2.start()
    m_self.wait()
    for k in range(4):
        m_wait(mr.at[0], m_prel.at[k])

    per = 128 // n_i

    def regroup(q, carry):
        k, c0 = q // (n_ch // 16), q % (n_ch // 16)
        blk = mr[pl.ds(per * k, per), :, pl.ds(pl.multiple_of(c0 * 16, 16), 16), :].astype(F32)
        blk = jnp.transpose(blk.reshape(128, 16, s_chip), (1, 0, 2))
        blk = jnp.transpose(blk, (0, 2, 1))
        mine = jnp.where(cc == 0, blk[:, 0:s_dev, :], blk[:, s_dev:, :])
        ov[k, :, pl.ds(pl.multiple_of(c0 * 16, 16), 16), :] = jnp.transpose(mine, (1, 0, 2)).astype(BF16)
        return carry

    lax.fori_loop(0, n_d // per * (n_ch // 16), regroup, 0)
    outs = [pltpu.make_async_copy(ov.at[k], mo_hbm.at[:, :, k * 128:(k + 1) * 128], sem_out.at[1 + k]) for k in range(n_d // per)]
    for o in outs:
        o.start()

    for cp in (b_r0, b_r1, b_l1, b_l0, b_fr, b_fl, m_or, m_ol, m_dr, m_dl, m_fr, m_fl, m_p0, m_p1, m_p2, m_p3):
        cp.wait_send()
    for u in (0, 2, 4, 6):
        for p in range(2):
            b_rel(u, p).wait_send()

    def drain(t, carry):
        for f in range(2):
            y1(t, f).wait_send()
            y2(t, f).wait_send()
        return carry

    lax.fori_loop(0, 8, drain, 0)
    out_z.wait()
    for o in outs:
        o.wait()


def solution(mesh):
    n_y, n_d = mesh.shape["seq"], mesh.shape["dap"]
    rep = P()
    in_specs = (P(("data", "seq"), "dap", None), P("data", None), P(("data", "dap"), None, None)) + (rep,) * 8
    out_specs = (P(("data", "dap"), None, None), P(("data", "seq", "dap"), None, None))

    def local_fn(m, mask, z, gamma, beta, w_l, b_l, w_r, b_r, w_o, b_o):
        s_loc, n_i, n_ch = m.shape
        s_all, n_j = mask.shape
        n_e = w_o.shape[1]
        c_hid = w_l.shape[1]
        half = n_i // 2
        hrows = half * c_hid
        s_dev = s_loc // n_d
        vecs = jnp.stack([jnp.pad(v.astype(F32), (0, n_e - v.shape[0])) for v in (gamma, beta, b_l, b_r, b_o)])
        any_spec = pl.BlockSpec(memory_space=pl.ANY)
        vm = pl.BlockSpec(memory_space=pltpu.VMEM)
        dma = pltpu.SemaphoreType.DMA
        ysh = (8, 2, half, n_i, n_e)
        z_out, m_out = pl.pallas_call(
            functools.partial(kernel, (n_y, n_d)),
            out_shape=(jax.ShapeDtypeStruct(z.shape, F32), jax.ShapeDtypeStruct((s_dev, n_ch, n_j), BF16)),
            in_specs=[any_spec] * 3 + [vm] * 4,
            out_specs=(any_spec, any_spec),
            scratch_shapes=[
                pltpu.VMEM((n_i, n_ch, s_loc), BF16),
                pltpu.VMEM((s_all, n_j), jnp.int32),
                pltpu.VMEM(z.shape, F32),
                pltpu.VMEM((n_i * n_ch, s_loc), BF16),
                pltpu.VMEM((hrows, half * n_ch), BF16),
                pltpu.VMEM((2, hrows, n_i), BF16),
                pltpu.VMEM((n_i, s_loc), F32),
                pltpu.VMEM((4, s_loc, 256), BF16),
                pltpu.VMEM((8, 2, hrows, s_loc), BF16),
                pltpu.VMEM((c_hid * 128, 4 * n_e), BF16),
                pltpu.VMEM((16, half, c_hid * 128), BF16),
                pltpu.VMEM(ysh, BF16),
                pltpu.VMEM(ysh, BF16),
                pltpu.VMEM(ysh, BF16),
                pltpu.VMEM(ysh, BF16),
                pltpu.VMEM((n_j, 128), F32),
                pltpu.VMEM((n_d, n_i, n_ch, s_loc * 2 // n_d), BF16),
                pltpu.VMEM((2, half, n_ch, s_loc * 2 // n_d), BF16),
                pltpu.VMEM((n_j // 128, s_dev, n_ch, 128), BF16),
                dma((4,)), dma((3,)), dma((4,)), dma((2,)), dma((8, 2)), dma((8, 2)),
                dma((2,)), dma((2,)), dma((2,)), dma((4,)), dma((4,)), dma((2,)), dma((4,)),
                dma((8, 2)), dma((8, 2)), dma((8, 2)), dma((8, 2)),
            ],
            compiler_params=pltpu.CompilerParams(collective_id=0, has_side_effects=True, vmem_limit_bytes=63 * 2**20),
            name="opm",
        )(jnp.transpose(m, (1, 2, 0)), mask, z, vecs, w_l.T, w_r.T, w_o)
        return z_out, jnp.transpose(m_out, (0, 2, 1))

    return jax.shard_map(local_fn, mesh=mesh, in_specs=in_specs, out_specs=out_specs, check_vma=False)
```

time: 345 us -> 90 us (0.26)
  waiting for transfers between devices: 166 us -> 0 us
  matrix products: 84 us -> 0 us
  Pallas kernels: 0 us -> 80.4 us
  other arithmetic: 38 us -> 0.6 us
  local copies, waits for them, and re-layouts: 35.3 us -> 8.16 us
  between operations: 14.3 us -> 0.65 us
  starting transfers between devices: 6.08 us -> 0 us
    reduce_scatter x1 -> x0, waiting for transfers between devices: 90.4 us -> none  [local_fn(): summed = lax.psum_scatter(partial, 'dap', scatter_dimension=0, tiled=True)]
    dot_general x7 -> x0, matrix products: 84 us -> none  [the longest x4 80.4 us: one_block(): jnp.einsum('icjd,cde->ije', outer_blk, w_out3, preferred_element_type=jnp...]
    pallas_call x0 -> x1, Pallas kernels: none -> 80.4 us  [local_fn(): pl.pallas_call(functools.partial(kernel, (n_y, n_d)), out_shape=(jax.Shap...]
    psum x1 -> x0, waiting for transfers between devices: 50.1 us -> none  [local_fn(): summed = lax.psum(summed, 'seq')]
    all_to_all x1 -> x0, waiting for transfers between devices: 25 us -> none  [local_fn(): local_c7 = lax.all_to_all(array_b7, 'dap', 0, 1, tiled=True)]
    unnamed x25 -> x4, local copies, waits for them, and re-layouts: 25.4 us -> 6.13 us
    convert_element_type x9 -> x0, other arithmetic: 13.5 us -> none  [the longest x1 12.2 us: layer_norm(): (normed * ln_gamma.astype(jnp.float32) + ln_beta.astype(jnp.float32)).ast...]
    reduce_sum x2 -> x0, other arithmetic: 10.6 us -> none  [the longest x1 6.18 us: layer_norm(): var_val = jnp.mean(centered * centered, axis=-1, keepdims=True)]
  transfers between devices with their start and end apart: 3 -> 0, of which waited for: 3 -> 0; matrix products, arithmetic and copies ran while one was open for 2% -> 0% of each run, Pallas kernels for 0% -> 0%
where the time goes in v1:
time: 90 us; the launch traced here: 89.8 us
  Pallas kernels  80.4 us (89%)
  local copies, waits for them, and re-layouts  8.16 us (9%)
    pallas_call x1, Pallas kernels, local_fn(): pl.pallas_call(functools.partial(kernel, (n_y, n_d)), out_shape=(jax.Shap...  80.4 us
    unnamed x4, local copies, waits for them, and re-layouts  6.13 us
    another operation x3, local copies, waits for them, and re-layouts, local_fn(): jnp.stack([jnp.pad(v.astype(F32), (0, n_e - v.shape[0])) for v in (gamma,...  2.04 us

profile of v1, /device:TPU:97, one launch (start us, length us, event | category | flops | bytes accessed | tf_op | source)
XLA Modules:
  0.0 89.8 jit_solution(10665411158342295747)
XLA Ops:
  0.6 0.7 pad_bitcast_fusion.2
  1.3 0.7 pad_bitcast_fusion
  2.0 0.7 stack.30
  2.7 0.6 stack.31.vecs
  3.3 80.4 %opm.1 = (f32[32,256,128]{2,1,0:T(8,128)}, bf16[64,64,256]{2,1,0:T(8,128)(2,1)}) custom-call(bf16[32,64,512]{2,1,0:T(8,128)(2,1)} %bitcast.14, s32[2048,256]{1,0:T(8,128)} %mask_hbm.1, f32[32,256,128]{2,1,0:T(8,128)} %z_hbm.1, f32[5,128]{1,0:T(8,128)} %stack.31.vecs, bf16[32,64]{1,0:T(8,128)(2,1)} %bitcast.15, bf16[32,64]{1,0:T(8,128)(2,1)} %bitcast.16, ...), custom_call_target="tpu_custom_call" | custom-call | tf_op jit(solution)/shard_map/opm/pallas_call | solution.py:408
  83.7 0.0 copy-start
  83.7 4.8 %copy.15 = f32[32,256,128]{2,1,0:T(8,128)} copy(f32[32,256,128]{2,1,0:T(8,128)} %get-tuple-element.12) | data formatting | bytes 8388608
  88.5 0.0 copy-done
  88.5 1.3 %copy.16 = bf16[64,256,64]{1,2,0:T(8,128)(2,1)} copy(bf16[64,256,64]{1,2,0:T(8,128)(2,1)S(1)} %bitcast.13) | data formatting | bytes 4194304
Async XLA Ops:
  83.7 4.8 %copy-start = (bf16[64,64,256]{2,1,0:T(8,128)(2,1)S(1)}, bf16[64,64,256]{2,1,0:T(8,128)(2,1)}, u32[]{:S(2)}) copy-start(bf16[64,64,256]{2,1,0:T(8,128)(2,1)} %get-tuple-element.5) | copy-start | bytes 6291460

commit v2 on v1

v2 whole, which is shorter than its diff:
```python
import functools
import jax
import jax.numpy as jnp
from jax import lax
from jax.experimental import pallas as pl
from jax.experimental.pallas import tpu as pltpu
from jax.sharding import PartitionSpec as P

F32 = jnp.float32
BF16 = jnp.bfloat16
VM_LIM = 56
LAG1 = 1
LAG2 = 2


def iota(shape, dim):
    return lax.broadcasted_iota(jnp.int32, shape, dim)


def onehot(cond):
    return jnp.where(cond, 1.0, 0.0).astype(BF16)


def dot(a, b):
    return jnp.dot(a, b, preferred_element_type=F32)


def dot_nt(a, b):
    return lax.dot_general(a, b, (((1,), (1,)), ((), ())), preferred_element_type=F32)


def dot_tn(a, b):
    return lax.dot_general(a, b, (((0,), (0,)), ((), ())), preferred_element_type=F32)


def kernel(dims, m_hbm, mask_hbm, z_hbm, gam, bet, bias_l, bias_r, bias_o, waT, wbT, wo, zv, ov,
           mT, mkv, mkl, xT, wbig, bbb, mkT, acat, bT, wblk, lbuf, rp, rq, sp, sq, rc, mr, tbuf,
           sem_in, bs_own, bs_fwd, bs_rel, b_recv, ms_dir, ms_opp, ms_fwd, ms_rel, m_recv, mf_recv, m_prel,
           y1s, y1r, y2s, y2r):
    n_y, n_d = dims
    n_x = n_d // 2
    yy = lax.axis_index("seq")
    dd = lax.axis_index("dap")
    xx = dd // 2
    cc = dd % 2
    x_r = (xx + 1) % n_x
    x_l = (xx + n_x - 1) % n_x
    x_o = (xx + 2) % n_x
    right, left, mate = 2 * x_r + cc, 2 * x_l + cc, 2 * xx + 1 - cc
    par = yy % 2
    y_a = yy + 1 - 2 * par
    y_b = (yy + n_y - 1 + 2 * par) % n_y
    n_i, n_ch, s_loc = mT.shape
    s_all, n_j = mkv.shape
    c_hid = waT.shape[0]
    half = n_i // 2
    hrows = half * c_hid
    s_chip = s_loc // n_x
    s_dev = s_loc // n_d

    def to_dap(idx):
        return dict(device_id={"dap": idx}, device_id_type=pl.DeviceIdType.MESH)

    def to_seq(idx):
        return dict(device_id={"seq": idx}, device_id_type=pl.DeviceIdType.MESH)

    in_m = pltpu.make_async_copy(m_hbm, mT, sem_in.at[0])
    mine_rows = pl.ds(pl.multiple_of(yy * s_loc, s_loc), s_loc)
    in_mloc = pltpu.make_async_copy(mask_hbm.at[mine_rows], mkl, sem_in.at[4])
    in_mask = pltpu.make_async_copy(mask_hbm, mkv, sem_in.at[1])
    in_z = pltpu.make_async_copy(z_hbm, zv, sem_in.at[2])
    in_mloc.start()
    in_m.start()

    barrier = pltpu.get_barrier_semaphore()
    for nb in (right, left, mate):
        pl.semaphore_signal(barrier, inc=1, **to_dap(nb))
    for nb in (y_a, y_b):
        pl.semaphore_signal(barrier, inc=1, **to_seq(nb))

    def remote(src, dst, ssem, rsem, to):
        return pltpu.make_async_remote_copy(src_ref=src, dst_ref=dst, send_sem=ssem, recv_sem=rsem, **to)

    def b_to(src_u, src_p, dst_u, dst_p, ssem, nb):
        return remote(bT.at[src_u, src_p], bT.at[dst_u, dst_p], ssem, b_recv.at[dst_u, dst_p], to_dap(nb))

    b_r0 = b_to(0, 0, 2, 0, bs_own.at[0], right)
    b_r1 = b_to(0, 1, 4, 0, bs_own.at[1], right)
    b_l1 = b_to(0, 1, 2, 1, bs_own.at[2], left)
    b_l0 = b_to(0, 0, 4, 1, bs_own.at[3], left)
    b_fr = b_to(2, 0, 6, 0, bs_fwd.at[0], right)
    b_fl = b_to(2, 1, 6, 1, bs_fwd.at[1], left)

    def b_rel(u, p):
        return b_to(u, p, u + 1, p, bs_rel.at[u, p], mate)

    def b_wait(u, p):
        b_to(u, p, u, p, bs_rel.at[u, p], mate).wait_recv()

    def lanes_of(xc):
        return pl.ds(pl.multiple_of(xc * s_chip, s_chip), s_chip)

    d_right, d_left, d_opp = 2 * x_r + cc, 2 * x_l + cc, 2 * x_o + cc
    up, lo = pl.ds(0, half), pl.ds(half, half)
    m_or = remote(m_hbm.at[up, :, lanes_of(x_o)], tbuf.at[0], ms_opp.at[0], mf_recv.at[0], to_dap(right))
    m_ol = remote(m_hbm.at[lo, :, lanes_of(x_o)], tbuf.at[1], ms_opp.at[1], mf_recv.at[1], to_dap(left))
    m_dr = remote(m_hbm.at[:, :, lanes_of(x_r)], mr.at[dd], ms_dir.at[0], m_recv.at[0], to_dap(right))
    first, rest = pl.ds(0, n_i // 4), pl.ds(n_i // 4, n_i - n_i // 4)
    m_dl0 = remote(m_hbm.at[first, :, lanes_of(x_l)], mr.at[dd, first], ms_dir.at[2], m_recv.at[4], to_dap(left))
    m_dl = remote(m_hbm.at[rest, :, lanes_of(x_l)], mr.at[dd, rest], ms_dir.at[1], m_recv.at[1], to_dap(left))
    m_fr = remote(tbuf.at[0], mr.at[d_left, up], ms_fwd.at[0], m_recv.at[2], to_dap(right))
    m_fl = remote(tbuf.at[1], mr.at[d_right, lo], ms_fwd.at[1], m_recv.at[3], to_dap(left))
    m_p0 = remote(m_hbm.at[:, :, lanes_of(xx)], mr.at[dd], ms_rel.at[0], m_prel.at[0], to_dap(mate))
    m_p1 = remote(mr.at[d_left], mr.at[d_left], ms_rel.at[1], m_prel.at[1], to_dap(mate))
    m_p2 = remote(mr.at[d_right], mr.at[d_right], ms_rel.at[2], m_prel.at[2], to_dap(mate))
    m_p3 = remote(mr.at[d_opp], mr.at[d_opp], ms_rel.at[3], m_prel.at[3], to_dap(mate))
    m_self = pltpu.make_async_copy(m_hbm.at[:, :, lanes_of(xx)], mr.at[dd], sem_in.at[3])

    def m_wait(ref, sem):
        remote(ref, ref, ms_rel.at[0], sem, to_dap(mate)).wait_recv()

    pl.semaphore_wait(barrier, 5)
    m_or.start()
    m_ol.start()
    m_dl0.start()
    m_p0.start()

    def column(row, n, wide):
        eye = iota((n, n), 0) == iota((n, n), 1)
        diag = jnp.where(eye, jnp.broadcast_to(row, (n, n)), 0.0).astype(BF16)
        return dot(diag, jnp.ones((n, wide), BF16))

    lw = s_loc // 2
    gcol = column(gam[...].astype(F32), n_ch, lw)
    bcol = column(bet[...].astype(F32), n_ch, lw)
    blc = column(bias_l[...].astype(F32), c_hid, 128)
    brc = column(bias_r[...].astype(F32), c_hid, 128)
    kb = half * n_ch
    wide = dot(wbT[...], onehot((iota((n_ch, kb), 1) & (n_ch - 1)) == iota((n_ch, kb), 0)))
    keep = iota((half, kb), 0) == iota((half, kb), 1) // n_ch
    lane_i = iota((half, n_i), 1) - iota((half, n_i), 0)
    for d in range(c_hid):
        rows = slice(d * half, (d + 1) * half)
        wbig[rows, :] = jnp.where(keep, jnp.broadcast_to(wide[d:d + 1, :], (half, kb)), 0.0).astype(BF16)
        bias = jnp.broadcast_to(brc[d:d + 1, 0:n_i], (half, n_i))
        for h in range(2):
            bbb[h, rows, :] = jnp.where(lane_i == h * half, bias, 0.0).astype(BF16)

    in_mloc.wait()
    selT = onehot(iota((n_i, n_j), 1) == iota((n_i, n_j), 0) + dd * n_i)
    mkT[...] = dot_nt(selT, mkl[...].astype(F32).astype(BF16))
    in_m.wait()

    ga = 128 // c_hid
    n_e = wo.shape[1]
    pos = iota((128, c_hid * c_hid), 0)
    want = (pos & (c_hid - 1)) * c_hid + pos // c_hid
    gap = iota((128, c_hid * c_hid), 1) - want

    def place(dc, carry):
        wp = dot(onehot(gap == dc * ga), wo[...]).astype(BF16)
        for k in range(ga):
            for i4 in range(ga):
                row = pl.multiple_of((dc * ga + k) * 128 + i4 * c_hid, c_hid)
                wblk[pl.ds(row, c_hid), i4 * n_e:(i4 + 1) * n_e] = wp[k * c_hid:(k + 1) * c_hid, :]
        return carry

    def norm_row(r, carry):
        for q in range(2):
            lanes = slice(q * lw, (q + 1) * lw)
            act = mT[r, :, lanes].astype(F32)
            mean = jnp.sum(act, axis=0, keepdims=True) * (1.0 / n_ch)
            cen = act - mean
            var = jnp.sum(cen * cen, axis=0, keepdims=True) * (1.0 / n_ch)
            nrm = cen * lax.rsqrt(var + 1e-5)
            val = (nrm * gcol + bcol).astype(BF16) * mkT[pl.ds(r, 1), lanes].astype(BF16)
            xT[pl.ds(pl.multiple_of(r * n_ch, n_ch), n_ch), lanes] = val
        return carry

    mk16 = mkT[...].astype(BF16)
    for h in range(2):
        lax.fori_loop(h * half, (h + 1) * half, norm_row, 0, unroll=2)
        acc = dot(wbig[...], xT[h * kb:(h + 1) * kb, :]) + dot(bbb[h], mk16)
        bT[0, h] = acc.astype(BF16)
        if h == 0:
            b_r0.start()
        else:
            b_l1.start()
            b_l0.start()
            b_r1.start()
        b_rel(0, h).start()
    m_self.start()
    in_mask.start()
    in_z.start()

    ka = ga * n_ch
    ra = onehot((iota((128, c_hid), 0) & (c_hid - 1)) == iota((128, c_hid), 1))
    wa_rep = dot(dot(ra, waT[...]).astype(BF16), onehot((iota((n_ch, ka), 1) & (n_ch - 1)) == iota((n_ch, ka), 0)))
    wa4 = jnp.where(iota((128, ka), 0) // c_hid == iota((128, ka), 1) // n_ch, wa_rep, 0.0).astype(BF16)
    ba_rep = dot(ra, blc.astype(BF16))[:, 0:n_i]
    lane_a = iota((128, n_i), 1) - iota((128, n_i), 0) // c_hid
    n_g = n_i // ga
    for g in range(n_g):
        bag = jnp.where(lane_a == ga * g, ba_rep, 0.0).astype(BF16)
        at = dot(wa4, xT[g * ka:(g + 1) * ka, :]) + dot(bag, mk16)
        acat[g // 2, :, (g % 2) * 128:(g % 2 + 1) * 128] = at.T.astype(BF16)

    wblk[...] = jnp.zeros_like(wblk)
    lax.fori_loop(0, c_hid // ga, place, 0, unroll=4)

    def pair_counts():
        sel = onehot(iota((n_j, 128), 0) == iota((n_j, 128), 1) + dd * n_i)
        rc[...] = jnp.zeros_like(rc)

        def add(k, carry):
            mk = mkv[pl.ds(pl.multiple_of(k * s_loc, s_loc), s_loc), :].astype(F32).astype(BF16)
            rc[...] += dot_tn(mk, dot(mk, sel).astype(BF16))
            return carry

        lax.fori_loop(0, s_all // s_loc, add, 0, unroll=2)
        rc[...] = 1.0 / (1e-3 + rc[...])

    def compute(t):
        lhs = bT[t].reshape(2 * hrows, s_loc)
        for n in range(4):
            acc = dot(lhs, acat[n]).astype(BF16)
            for h in range(2):
                for d in range(c_hid):
                    row = (h * c_hid + d) * half
                    for gg in range(2):
                        lbuf[(2 * n + gg) * 2 + h, :, d * 128:(d + 1) * 128] = acc[row:row + half, gg * 128:(gg + 1) * 128]
        for nn in range(2):
            cols = slice(nn * 256, (nn + 1) * 256)
            res = dot(lbuf[...].reshape(n_g * n_i, c_hid * 128), wblk[:, cols]).astype(BF16)
            for g in range(n_g):
                for k in range(2):
                    i = ga * g + 2 * nn + k
                    rp[t, i // half, i % half] = res[g * n_i:(g + 1) * n_i, k * 128:(k + 1) * 128]

    def y1(t, f):
        return remote(rp.at[t, f], rq.at[t, f], y1s.at[t, f], y1r.at[t, f], to_seq(y_a if f == 0 else y_b))

    def y2(t, f):
        return remote(sp.at[t, f], sq.at[t, f], y2s.at[t, f], y2r.at[t, f], to_seq(y_b if f == 0 else y_a))

    def j_of(t, p):
        u = t // 2
        off = jnp.where(u == 0, 0, jnp.where(u == 3, 2, n_x - 1 if p == 0 else 1))
        core = jnp.where(t % 2 == 0, cc, 1 - cc)
        hh = jnp.where(u == 2, 1 - p, p)
        return pl.multiple_of((2 * ((xx + off) % n_x) + core) * n_i + hh * half, half)

    def finish(t):
        bo = bias_o[...].astype(F32)
        for f in range(2):
            y2(t, f).wait_recv()
        for p in range(2):
            j0 = j_of(t, p)
            rcp = rc[pl.ds(j0, half), :]
            for i in range(n_i):
                rows = slice(p * half, (p + 1) * half)
                tot = sp[t, i // half, i % half, rows, :].astype(F32) + sq[t, i // half, i % half, rows, :].astype(F32)
                upd = (tot + bo) * jnp.broadcast_to(rcp[:, i:i + 1], (half, n_e))
                zv[i, pl.ds(j0, half), :] += upd

    per = 128 // n_i

    def regroup(k):
        def part(c0, carry):
            chs = pl.ds(pl.multiple_of(c0 * 16, 16), 16)
            blk = mr[pl.ds(per * k, per), :, chs, :].astype(F32)
            blk = jnp.transpose(blk.reshape(128, 16, s_chip), (1, 0, 2))
            blk = jnp.transpose(blk, (0, 2, 1))
            mine = jnp.where(cc == 0, blk[:, 0:s_dev, :], blk[:, s_dev:, :])
            ov[:, chs, pl.ds(pl.multiple_of(k * 128, 128), 128)] = jnp.transpose(mine, (1, 0, 2)).astype(BF16)
            return carry

        lax.fori_loop(0, n_ch // 16, part, 0)

    def step(t, carry):
        @pl.when(t == 1)
        def _():
            b_wait(1, 0)
            b_wait(1, 1)

        @pl.when(t == 2)
        def _():
            in_mask.wait()
            in_z.wait()
            pair_counts()
            b_wait(2, 0)
            b_fr.start()
            b_rel(2, 0).start()
            b_wait(2, 1)
            b_fl.start()
            b_rel(2, 1).start()
            m_dr.start()
            m_dl.start()
            m_wait(tbuf.at[0], mf_recv.at[0])
            m_fr.start()
            m_wait(tbuf.at[1], mf_recv.at[1])
            m_fl.start()

        @pl.when(t == 3)
        def _():
            b_wait(3, 0)
            b_wait(3, 1)

        @pl.when(t == 4)
        def _():
            b_wait(4, 0)
            b_rel(4, 0).start()
            b_wait(4, 1)
            b_rel(4, 1).start()

        @pl.when(t == 5)
        def _():
            b_wait(5, 0)
            b_wait(5, 1)

        @pl.when(t == 6)
        def _():
            b_wait(6, 0)
            b_rel(6, 0).start()
            b_wait(6, 1)
            b_rel(6, 1).start()

        @pl.when(t == 7)
        def _():
            b_wait(7, 0)
            b_wait(7, 1)

        @pl.when(t < 8)
        def _():
            compute(t)
            for f in range(2):
                y1(t, f).start()

        @pl.when(jnp.logical_and(t >= LAG1, t < 8 + LAG1))
        def _():
            v = t - LAG1
            for f in range(2):
                y1(v, f).wait_recv()

                def add(i, carry):
                    tot = rp[v, f, i].astype(F32) + rq[v, f, i].astype(F32)
                    sp[v, f, i] = tot.astype(BF16)
                    return carry

                lax.fori_loop(0, half, add, 0, unroll=4)
                y2(v, f).start()

        @pl.when(t >= LAG2)
        def _():
            finish(t - LAG2)

        @pl.when(t == 6 + LAG2)
        def _():
            m_wait(mr.at[d_left, rest], m_recv.at[1])
            m_wait(mr.at[d_left, first], m_recv.at[4])
            m_wait(mr.at[d_right], m_recv.at[0])
            m_p1.start()
            m_p2.start()
            m_self.wait()
            for k in range(3):
                m_wait(mr.at[0], m_prel.at[k])
            regroup(xx // 2)

        @pl.when(t == 7 + LAG2)
        def _():
            m_wait(mr.at[d_opp, up], m_recv.at[2])
            m_wait(mr.at[d_opp, lo], m_recv.at[3])
            m_p3.start()
            m_wait(mr.at[0], m_prel.at[3])
            regroup(1 - xx // 2)

        return carry

    lax.fori_loop(0, 8 + LAG2, step, 0)

    for cp in (b_r0, b_r1, b_l1, b_l0, b_fr, b_fl, m_or, m_ol, m_dr, m_dl0, m_dl, m_fr, m_fl, m_p0, m_p1, m_p2, m_p3):
        cp.wait_send()
    for u in (0, 2, 4, 6):
        for p in range(2):
            b_rel(u, p).wait_send()

    def drain(t, carry):
        for f in range(2):
            y1(t, f).wait_send()
            y2(t, f).wait_send()
        return carry

    lax.fori_loop(0, 8, drain, 0)


def solution(mesh):
    n_y, n_d = mesh.shape["seq"], mesh.shape["dap"]
    rep = P()
    in_specs = (P(("data", "seq"), "dap", None), P("data", None), P(("data", "dap"), None, None)) + (rep,) * 8
    out_specs = (P(("data", "dap"), None, None), P(("data", "seq", "dap"), None, None))

    def local_fn(m, mask, z, gamma, beta, w_l, b_l, w_r, b_r, w_o, b_o):
        s_loc, n_i, n_ch = m.shape
        s_all, n_j = mask.shape
        n_e = w_o.shape[1]
        c_hid = w_l.shape[1]
        half = n_i // 2
        hrows = half * c_hid
        s_dev = s_loc // n_d
        vecs = [v.reshape(1, -1) for v in (gamma, beta, b_l, b_r, b_o)]
        any_spec = pl.BlockSpec(memory_space=pl.ANY)
        vm = pl.BlockSpec(memory_space=pltpu.VMEM)
        dma = pltpu.SemaphoreType.DMA
        ysh = (8, 2, half, n_i, n_e)
        z_out, m_out = pl.pallas_call(
            functools.partial(kernel, (n_y, n_d)),
            out_shape=(pltpu.VMEM(z.shape, F32), pltpu.VMEM((s_dev, n_ch, n_j), BF16)),
            in_specs=[any_spec] * 3 + [vm] * 8,
            out_specs=(vm, vm),
            scratch_shapes=[
                pltpu.VMEM((n_i, n_ch, s_loc), BF16),
                pltpu.VMEM((s_all, n_j), jnp.int32),
                pltpu.VMEM((s_loc, n_j), jnp.int32),
                pltpu.VMEM((n_i * n_ch, s_loc), BF16),
                pltpu.VMEM((hrows, half * n_ch), BF16),
                pltpu.VMEM((2, hrows, n_i), BF16),
                pltpu.VMEM((n_i, s_loc), F32),
                pltpu.VMEM((4, s_loc, 256), BF16),
                pltpu.VMEM((8, 2, hrows, s_loc), BF16),
                pltpu.VMEM((c_hid * 128, 4 * n_e), BF16),
                pltpu.VMEM((16, half, c_hid * 128), BF16),
                pltpu.VMEM(ysh, BF16),
                pltpu.VMEM(ysh, BF16),
                pltpu.VMEM(ysh, BF16),
                pltpu.VMEM(ysh, BF16),
                pltpu.VMEM((n_j, 128), F32),
                pltpu.VMEM((n_d, n_i, n_ch, s_loc * 2 // n_d), BF16),
                pltpu.VMEM((2, half, n_ch, s_loc * 2 // n_d), BF16),
                dma((5,)), dma((4,)), dma((2,)), dma((8, 2)), dma((8, 2)),
                dma((3,)), dma((2,)), dma((2,)), dma((4,)), dma((5,)), dma((2,)), dma((4,)),
                dma((8, 2)), dma((8, 2)), dma((8, 2)), dma((8, 2)),
            ],
            compiler_params=pltpu.CompilerParams(collective_id=0, has_side_effects=True, vmem_limit_bytes=VM_LIM * 2**20),
            name="opm",
        )(jnp.transpose(m, (1, 2, 0)), mask, z, *vecs, w_l.T, w_r.T, w_o)
        return z_out, jnp.transpose(m_out, (0, 2, 1))

    return jax.shard_map(local_fn, mesh=mesh, in_specs=in_specs, out_specs=out_specs, check_vma=False)
```

time: 90 us -> 80.7 us (0.90)
  local copies, waits for them, and re-layouts: 8.16 us -> 3.33 us
  Pallas kernels: 80.4 us -> 76.2 us
    pallas_call x1, Pallas kernels: 80.4 us -> 76.2 us  [local_fn(): pl.pallas_call(functools.partial(kernel, (n_y, n_d)), out_shape=(pltpu.VM...]
    unnamed x4 -> x2, local copies, waits for them, and re-layouts: 6.13 us -> 3.33 us
    another operation x3 -> x0, local copies, waits for them, and re-layouts: 2.04 us -> none  [local_fn(): jnp.stack([jnp.pad(v.astype(F32), (0, n_e - v.shape[0])) for v in (gamma,...]
where the time goes in v2:
time: 80.7 us; the launch traced here: 80.1 us
  Pallas kernels  76.2 us (94%)
  local copies, waits for them, and re-layouts  3.33 us (4%)
    pallas_call x1, Pallas kernels, local_fn(): pl.pallas_call(functools.partial(kernel, (n_y, n_d)), out_shape=(pltpu.VM...  76.2 us
    unnamed x2, local copies, waits for them, and re-layouts  3.33 us

profile of v2, /device:TPU:97, one launch (start us, length us, event | category | flops | bytes accessed | tf_op | source)
XLA Modules:
  0.0 80.1 jit_solution(14898922741771768092)
XLA Ops:
  0.6 76.2 %opm.1 = (f32[32,256,128]{2,1,0:T(8,128)S(1)}, bf16[64,64,256]{2,1,0:T(8,128)(2,1)S(1)}) custom-call(bf16[32,64,512]{2,1,0:T(8,128)(2,1)} %bitcast.10, s32[2048,256]{1,0:T(8,128)} %mask_hbm.1, f32[32,256,128]{2,1,0:T(8,128)} %z_hbm.1, bf16[1,64]{1,0:T(2,128)(2,1)} %bitcast.13, bf16[1,64]{1,0:T(2,128)(2,1)} %bitcast.14, bf16[1,32]{1,0:T(2,128)(2,1)} %bitcast.15, ...), custom_call_target="tpu_custom_call" | custom-call | tf_op jit(solution)/shard_map/opm/pallas_call | solution.py:415
  76.8 2.0 %copy.15 = f32[32,256,128]{2,1,0:T(8,128)} copy(f32[32,256,128]{2,1,0:T(8,128)S(1)} %get-tuple-element.6) | data formatting | bytes 8388608
  78.8 1.3 %copy.16 = bf16[64,256,64]{1,2,0:T(8,128)(2,1)} copy(bf16[64,256,64]{1,2,0:T(8,128)(2,1)S(1)} %bitcast.9) | data formatting | bytes 4194304

commit v3 on v2

--- a/solution.py
+++ b/solution.py
@@ -8,7 +8,6 @@
 
 F32 = jnp.float32
 BF16 = jnp.bfloat16
-VM_LIM = 56
 LAG1 = 1
 LAG2 = 2
 
@@ -33,10 +32,41 @@
     return lax.dot_general(a, b, (((0,), (0,)), ((), ())), preferred_element_type=F32)
 
 
-def kernel(dims, m_hbm, mask_hbm, z_hbm, gam, bet, bias_l, bias_r, bias_o, waT, wbT, wo, zv, ov,
-           mT, mkv, mkl, xT, wbig, bbb, mkT, acat, bT, wblk, lbuf, rp, rq, sp, sq, rc, mr, tbuf,
-           sem_in, bs_own, bs_fwd, bs_rel, b_recv, ms_dir, ms_opp, ms_fwd, ms_rel, m_recv, mf_recv, m_prel,
-           y1s, y1r, y2s, y2r):
+def regroup(mr, k, chs, cc):
+    _, n_i, _, s_chip = mr.shape
+    per = 128 // n_i
+    blk = mr[per * k:per * (k + 1), :, chs, :].astype(F32)
+    blk = jnp.transpose(blk.reshape(128, blk.shape[2], s_chip), (1, 0, 2))
+    blk = jnp.transpose(blk, (0, 2, 1))
+    mine = jnp.where(cc == 0, blk[:, 0:s_chip // 2, :], blk[:, s_chip // 2:, :])
+    return jnp.transpose(mine, (1, 0, 2)).astype(BF16)
+
+
+def put_out(z_ref, o_ref, mr, zo_hbm, mo_hbm, last, sem):
+    cc = lax.axis_index("dap") % 2
+    n_z = z_ref.shape[0] // 4
+    n_ch = o_ref.shape[1]
+    ch_p = last.shape[1]
+    outs = [pltpu.make_async_copy(z_ref.at[k * n_z:(k + 1) * n_z], zo_hbm.at[k * n_z:(k + 1) * n_z], sem.at[k]) for k in range(4)]
+    outs.append(pltpu.make_async_copy(o_ref.at[:, 0:n_ch - ch_p], mo_hbm.at[:, 0:n_ch - ch_p], sem.at[4]))
+    for o in outs:
+        o.start()
+    for k in range(last.shape[2] // 128):
+        last[:, :, k * 128:(k + 1) * 128] = regroup(mr, k, pl.ds(n_ch - ch_p, ch_p), cc)
+    tail = pltpu.make_async_copy(last, mo_hbm.at[:, n_ch - ch_p:], sem.at[5])
+    tail.start()
+    for o in outs + [tail]:
+        o.wait()
+
+
+def kernel(dims, m_hbm, mask_hbm, z_hbm, *refs):
+    smalls_hbm, refs = refs[:8], refs[8:]
+    (zv, ov, mr), refs = refs[:3], refs[3:]
+    smalls, refs = refs[:8], refs[8:]
+    gam, bet, bias_l, bias_r, bias_o, waT, wbT, wo = smalls
+    (mT, mkv, mkl, xT, wbig, bbb, mkT, acat, bT, wblk, lbuf, rp, rq, sp, sq, rc, tbuf,
+     sem_in, sem_small, bs_own, bs_fwd, bs_rel, b_recv, ms_dir, ms_opp, ms_fwd, ms_rel, m_recv, mo_recv, mf_recv, m_prel,
+           y1s, y1r, y2s, y2r) = refs
     n_y, n_d = dims
     n_x = n_d // 2
     yy = lax.axis_index("seq")
@@ -69,14 +99,19 @@
     in_mloc = pltpu.make_async_copy(mask_hbm.at[mine_rows], mkl, sem_in.at[4])
     in_mask = pltpu.make_async_copy(mask_hbm, mkv, sem_in.at[1])
     in_z = pltpu.make_async_copy(z_hbm, zv, sem_in.at[2])
-    in_mloc.start()
-    in_m.start()
+
+    in_small = [pltpu.make_async_copy(a, b, sem_small.at[k]) for k, (a, b) in enumerate(zip(smalls_hbm, smalls))]
 
     barrier = pltpu.get_barrier_semaphore()
     for nb in (right, left, mate):
         pl.semaphore_signal(barrier, inc=1, **to_dap(nb))
     for nb in (y_a, y_b):
         pl.semaphore_signal(barrier, inc=1, **to_seq(nb))
+
+    in_m.start()
+    in_mloc.start()
+    for cp in in_small:
+        cp.start()
 
     def remote(src, dst, ssem, rsem, to):
         return pltpu.make_async_remote_copy(src_ref=src, dst_ref=dst, send_sem=ssem, recv_sem=rsem, **to)
@@ -104,27 +139,33 @@
     up, lo = pl.ds(0, half), pl.ds(half, half)
     m_or = remote(m_hbm.at[up, :, lanes_of(x_o)], tbuf.at[0], ms_opp.at[0], mf_recv.at[0], to_dap(right))
     m_ol = remote(m_hbm.at[lo, :, lanes_of(x_o)], tbuf.at[1], ms_opp.at[1], mf_recv.at[1], to_dap(left))
-    m_dr = remote(m_hbm.at[:, :, lanes_of(x_r)], mr.at[dd], ms_dir.at[0], m_recv.at[0], to_dap(right))
-    first, rest = pl.ds(0, n_i // 4), pl.ds(n_i // 4, n_i - n_i // 4)
-    m_dl0 = remote(m_hbm.at[first, :, lanes_of(x_l)], mr.at[dd, first], ms_dir.at[2], m_recv.at[4], to_dap(left))
-    m_dl = remote(m_hbm.at[rest, :, lanes_of(x_l)], mr.at[dd, rest], ms_dir.at[1], m_recv.at[1], to_dap(left))
-    m_fr = remote(tbuf.at[0], mr.at[d_left, up], ms_fwd.at[0], m_recv.at[2], to_dap(right))
-    m_fl = remote(tbuf.at[1], mr.at[d_right, lo], ms_fwd.at[1], m_recv.at[3], to_dap(left))
-    m_p0 = remote(m_hbm.at[:, :, lanes_of(xx)], mr.at[dd], ms_rel.at[0], m_prel.at[0], to_dap(mate))
-    m_p1 = remote(mr.at[d_left], mr.at[d_left], ms_rel.at[1], m_prel.at[1], to_dap(mate))
-    m_p2 = remote(mr.at[d_right], mr.at[d_right], ms_rel.at[2], m_prel.at[2], to_dap(mate))
-    m_p3 = remote(mr.at[d_opp], mr.at[d_opp], ms_rel.at[3], m_prel.at[3], to_dap(mate))
+    n_p = 4
+    ch_p = n_ch // n_p
+
+    def m_dir(k, p):
+        chs = pl.ds(pl.multiple_of(p * ch_p, ch_p), ch_p)
+        src = m_hbm.at[:, chs, lanes_of(x_l if k else x_r)]
+        return remote(src, mr.at[dd, :, chs], ms_dir.at[k, p], m_recv.at[k, p], to_dap(left if k else right))
+
+    def m_rel(k, p):
+        chs = pl.ds(pl.multiple_of(p * ch_p, ch_p), ch_p)
+        ref = mr.at[d_right if k == 0 else d_left, :, chs]
+        return remote(ref, ref, ms_rel.at[k, p], m_prel.at[k, p], to_dap(mate))
+
+    m_fr = remote(tbuf.at[0], mr.at[d_left, up], ms_fwd.at[0], mo_recv.at[0], to_dap(right))
+    m_fl = remote(tbuf.at[1], mr.at[d_right, lo], ms_fwd.at[1], mo_recv.at[1], to_dap(left))
+    m_p0 = remote(m_hbm.at[:, :, lanes_of(xx)], mr.at[dd], ms_rel.at[2, 0], m_prel.at[2, 0], to_dap(mate))
+    m_p3 = [remote(mr.at[d_opp, rows], mr.at[d_opp, rows], ms_rel.at[2, 1 + k], m_prel.at[2, 1 + k], to_dap(mate))
+            for k, rows in enumerate((up, lo))]
     m_self = pltpu.make_async_copy(m_hbm.at[:, :, lanes_of(xx)], mr.at[dd], sem_in.at[3])
-
-    def m_wait(ref, sem):
-        remote(ref, ref, ms_rel.at[0], sem, to_dap(mate)).wait_recv()
 
     pl.semaphore_wait(barrier, 5)
     m_or.start()
     m_ol.start()
-    m_dl0.start()
     m_p0.start()
 
+    for cp in in_small:
+        cp.wait()
     def column(row, n, wide):
         eye = iota((n, n), 0) == iota((n, n), 1)
         diag = jnp.where(eye, jnp.broadcast_to(row, (n, n)), 0.0).astype(BF16)
@@ -265,17 +306,18 @@
 
     per = 128 // n_i
 
-    def regroup(k):
-        def part(c0, carry):
-            chs = pl.ds(pl.multiple_of(c0 * 16, 16), 16)
-            blk = mr[pl.ds(per * k, per), :, chs, :].astype(F32)
-            blk = jnp.transpose(blk.reshape(128, 16, s_chip), (1, 0, 2))
-            blk = jnp.transpose(blk, (0, 2, 1))
-            mine = jnp.where(cc == 0, blk[:, 0:s_dev, :], blk[:, s_dev:, :])
-            ov[:, chs, pl.ds(pl.multiple_of(k * 128, 128), 128)] = jnp.transpose(mine, (1, 0, 2)).astype(BF16)
-            return carry
-
-        lax.fori_loop(0, n_ch // 16, part, 0)
+    def m_land(p):
+        for k in range(2):
+            m_dir(k, p).wait_recv()
+            m_rel(1 - k, p).start()
+
+    def m_part(p):
+        for k in range(2):
+            m_rel(k, p).wait_recv()
+        if p < n_p - 1:
+            chs = pl.ds(p * ch_p, ch_p)
+            for k in range(n_d // per):
+                ov[:, chs, k * 128:(k + 1) * 128] = regroup(mr, k, chs, cc)
 
     def step(t, carry):
         @pl.when(t == 1)
@@ -294,12 +336,13 @@
             b_wait(2, 1)
             b_fl.start()
             b_rel(2, 1).start()
-            m_dr.start()
-            m_dl.start()
-            m_wait(tbuf.at[0], mf_recv.at[0])
+            m_or.wait_recv()
             m_fr.start()
-            m_wait(tbuf.at[1], mf_recv.at[1])
+            m_ol.wait_recv()
             m_fl.start()
+            for p in range(n_p):
+                m_dir(0, p).start()
+                m_dir(1, p).start()
 
         @pl.when(t == 3)
         def _():
@@ -350,36 +393,40 @@
                 lax.fori_loop(0, half, add, 0, unroll=4)
                 y2(v, f).start()
 
+        @pl.when(t == 6 + LAG2)
+        def _():
+            m_self.wait()
+            for k in range(2):
+                m_fr.wait_recv() if k == 0 else m_fl.wait_recv()
+                m_p3[k].start()
+            m_land(0)
+            m_p0.wait_recv()
+            for k in range(2):
+                m_p3[k].wait_recv()
+            m_land(1)
+            m_part(0)
+
         @pl.when(t >= LAG2)
         def _():
             finish(t - LAG2)
 
-        @pl.when(t == 6 + LAG2)
-        def _():
-            m_wait(mr.at[d_left, rest], m_recv.at[1])
-            m_wait(mr.at[d_left, first], m_recv.at[4])
-            m_wait(mr.at[d_right], m_recv.at[0])
-            m_p1.start()
-            m_p2.start()
-            m_self.wait()
-            for k in range(3):
-                m_wait(mr.at[0], m_prel.at[k])
-            regroup(xx // 2)
-
         @pl.when(t == 7 + LAG2)
         def _():
-            m_wait(mr.at[d_opp, up], m_recv.at[2])
-            m_wait(mr.at[d_opp, lo], m_recv.at[3])
-            m_p3.start()
-            m_wait(mr.at[0], m_prel.at[3])
-            regroup(1 - xx // 2)
+            for p in range(2, n_p):
+                m_land(p)
+                m_part(p - 1)
+            m_part(n_p - 1)
 
         return carry
 
     lax.fori_loop(0, 8 + LAG2, step, 0)
 
-    for cp in (b_r0, b_r1, b_l1, b_l0, b_fr, b_fl, m_or, m_ol, m_dr, m_dl0, m_dl, m_fr, m_fl, m_p0, m_p1, m_p2, m_p3):
+    for cp in (b_r0, b_r1, b_l1, b_l0, b_fr, b_fl, m_or, m_ol, m_fr, m_fl, m_p0, *m_p3):
         cp.wait_send()
+    for k in range(2):
+        for p in range(n_p):
+            m_dir(k, p).wait_send()
+            m_rel(k, p).wait_send()
     for u in (0, 2, 4, 6):
         for p in range(2):
             b_rel(u, p).wait_send()
@@ -408,16 +455,18 @@
         hrows = half * c_hid
         s_dev = s_loc // n_d
         vecs = [v.reshape(1, -1) for v in (gamma, beta, b_l, b_r, b_o)]
+        smalls = (*vecs, w_l.T, w_r.T, w_o)
         any_spec = pl.BlockSpec(memory_space=pl.ANY)
         vm = pl.BlockSpec(memory_space=pltpu.VMEM)
         dma = pltpu.SemaphoreType.DMA
         ysh = (8, 2, half, n_i, n_e)
-        z_out, m_out = pl.pallas_call(
+        mr_shape = (n_d, n_i, n_ch, s_loc * 2 // n_d)
+        held = pl.pallas_call(
             functools.partial(kernel, (n_y, n_d)),
-            out_shape=(pltpu.VMEM(z.shape, F32), pltpu.VMEM((s_dev, n_ch, n_j), BF16)),
-            in_specs=[any_spec] * 3 + [vm] * 8,
-            out_specs=(vm, vm),
-            scratch_shapes=[
+            out_shape=(pltpu.VMEM(z.shape, F32), pltpu.VMEM((s_dev, n_ch, n_j), BF16), pltpu.VMEM(mr_shape, BF16)),
+            in_specs=[any_spec] * 11,
+            out_specs=(vm, vm, vm),
+            scratch_shapes=[pltpu.VMEM(v.shape, BF16) for v in smalls] + [
                 pltpu.VMEM((n_i, n_ch, s_loc), BF16),
                 pltpu.VMEM((s_all, n_j), jnp.int32),
                 pltpu.VMEM((s_loc, n_j), jnp.int32),
@@ -434,15 +483,23 @@
                 pltpu.VMEM(ysh, BF16),
                 pltpu.VMEM(ysh, BF16),
                 pltpu.VMEM((n_j, 128), F32),
-                pltpu.VMEM((n_d, n_i, n_ch, s_loc * 2 // n_d), BF16),
                 pltpu.VMEM((2, half, n_ch, s_loc * 2 // n_d), BF16),
-                dma((5,)), dma((4,)), dma((2,)), dma((8, 2)), dma((8, 2)),
-                dma((3,)), dma((2,)), dma((2,)), dma((4,)), dma((5,)), dma((2,)), dma((4,)),
+                dma((5,)), dma((8,)), dma((4,)), dma((2,)), dma((8, 2)), dma((8, 2)),
+                dma((2, 4)), dma((2,)), dma((2,)), dma((3, 4)), dma((2, 4)), dma((2,)), dma((2,)), dma((3, 4)),
                 dma((8, 2)), dma((8, 2)), dma((8, 2)), dma((8, 2)),
             ],
-            compiler_params=pltpu.CompilerParams(collective_id=0, has_side_effects=True, vmem_limit_bytes=VM_LIM * 2**20),
+            compiler_params=pltpu.CompilerParams(collective_id=0, has_side_effects=True, vmem_limit_bytes=52 * 2**20),
             name="opm",
-        )(jnp.transpose(m, (1, 2, 0)), mask, z, *vecs, w_l.T, w_r.T, w_o)
+        )(jnp.transpose(m, (1, 2, 0)), mask, z, *smalls)
+        z_out, m_out = pl.pallas_call(
+            put_out,
+            out_shape=(jax.ShapeDtypeStruct(z.shape, F32), jax.ShapeDtypeStruct((s_dev, n_ch, n_j), BF16)),
+            in_specs=[vm] * 3,
+            out_specs=(any_spec, any_spec),
+            scratch_shapes=[pltpu.VMEM((s_dev, n_ch // 4, n_j), BF16), dma((6,))],
+            compiler_params=pltpu.CompilerParams(vmem_limit_bytes=10 * 2**20),
+            name="out",
+        )(*held)
         return z_out, jnp.transpose(m_out, (0, 2, 1))
 
     return jax.shard_map(local_fn, mesh=mesh, in_specs=in_specs, out_specs=out_specs, check_vma=False)

time: 80.7 us -> 74 us (0.917)
  local copies, waits for them, and re-layouts: 3.33 us -> 0 us
  Pallas kernels: 76.2 us -> 73.2 us
    pallas_call x1, Pallas kernels: 76.2 us -> 70.5 us  [local_fn(): pl.pallas_call(functools.partial(kernel, (n_y, n_d)), out_shape=(pltpu.VM...]
    unnamed x2 -> x0, local copies, waits for them, and re-layouts: 3.33 us -> none
    pallas_call x0 -> x1, Pallas kernels: none -> 2.7 us  [local_fn(): pl.pallas_call(put_out, out_shape=(jax.ShapeDtypeStruct(z.shape, F32), ja...]
where the time goes in v3:
time: 74 us; the launch traced here: 73.9 us
  Pallas kernels  73.2 us (99%)
    pallas_call x1, Pallas kernels, local_fn(): pl.pallas_call(functools.partial(kernel, (n_y, n_d)), out_shape=(pltpu.VM...  70.5 us
    pallas_call x1, Pallas kernels, local_fn(): pl.pallas_call(put_out, out_shape=(jax.ShapeDtypeStruct(z.shape, F32), ja...  2.7 us

profile of v3, /device:TPU:97, one launch (start us, length us, event | category | flops | bytes accessed | tf_op | source)
XLA Modules:
  0.0 73.9 jit_solution(7868877663178995654)
XLA Ops:
  0.6 70.5 %opm.1 = (f32[32,256,128]{2,1,0:T(8,128)S(1)}, bf16[64,64,256]{2,1,0:T(8,128)(2,1)S(1)}, bf16[8,32,64,128]{3,2,1,0:T(8,128)(2,1)S(1)}) custom-call(bf16[32,64,512]{2,1,0:T(8,128)(2,1)} %bitcast.9, s32[2048,256]{1,0:T(8,128)} %mask_hbm.1, f32[32,256,128]{2,1,0:T(8,128)} %z_hbm.1, bf16[1,64]{1,0:T(2,128)(2,1)} %bitcast.12, bf16[1,64]{1,0:T(2,128)(2,1)} %bitcast.13, ...), custom_call_target="tpu_custom_call" | custom-call | tf_op jit(solution)/shard_map/opm/pallas_call | solution.py:464
  71.2 2.7 %out.1 = (f32[32,256,128]{2,1,0:T(8,128)}, bf16[64,64,256]{2,1,0:T(8,128)(2,1)}) custom-call(f32[32,256,128]{2,1,0:T(8,128)S(1)} %get-tuple-element.7.z_ref, bf16[64,64,256]{2,1,0:T(8,128)(2,1)S(1)} %get-tuple-element.8.o_ref, bf16[8,32,64,128]{3,2,1,0:T(8,128)(2,1)S(1)} %get-tuple-element.9.mr), custom_call_target="tpu_custom_call" | custom-call | tf_op jit(solution)/shard_map/out/pallas_call | solution.py:494

commit v4 on v3

--- a/solution.py
+++ b/solution.py
@@ -9,7 +9,7 @@
 F32 = jnp.float32
 BF16 = jnp.bfloat16
 LAG1 = 1
-LAG2 = 2
+LAG2 = 3
 
 
 def iota(shape, dim):
@@ -64,8 +64,8 @@
     (zv, ov, mr), refs = refs[:3], refs[3:]
     smalls, refs = refs[:8], refs[8:]
     gam, bet, bias_l, bias_r, bias_o, waT, wbT, wo = smalls
-    (mT, mkv, mkl, xT, wbig, bbb, mkT, acat, bT, wblk, lbuf, rp, rq, sp, sq, rc, tbuf,
-     sem_in, sem_small, bs_own, bs_fwd, bs_rel, b_recv, ms_dir, ms_opp, ms_fwd, ms_rel, m_recv, mo_recv, mf_recv, m_prel,
+    (mT, mkv, mkl, xT, wbig, bbb, mkT, acat, bT, wblk, lbuf, rp, rq, sp, sq, rc, tbuf, gb, mko,
+     sem_in, sem_small, bs_own, bs_fwd, bs_rel, b_recv, bs_cut, bc_recv, ms_dir, ms_opp, ms_fwd, ms_rel, m_recv, mo_recv, mf_recv, m_prel,
            y1s, y1r, y2s, y2r) = refs
     n_y, n_d = dims
     n_x = n_d // 2
@@ -116,12 +116,20 @@
     def remote(src, dst, ssem, rsem, to):
         return pltpu.make_async_remote_copy(src_ref=src, dst_ref=dst, send_sem=ssem, recv_sem=rsem, **to)
 
+    def lanes_of(xc):
+        return pl.ds(pl.multiple_of(xc * s_chip, s_chip), s_chip)
+
     def b_to(src_u, src_p, dst_u, dst_p, ssem, nb):
         return remote(bT.at[src_u, src_p], bT.at[dst_u, dst_p], ssem, b_recv.at[dst_u, dst_p], to_dap(nb))
 
-    b_r0 = b_to(0, 0, 2, 0, bs_own.at[0], right)
+    n_f = n_x - 1
+
+    def b_cut(p, k):
+        cols = lanes_of((x_o + 1 + k) % n_x)
+        src, dst = bT.at[0, p, :, cols], bT.at[2, p, :, cols]
+        return remote(src, dst, bs_cut.at[p, k], bc_recv.at[p, k], to_dap(left if p else right))
+
     b_r1 = b_to(0, 1, 4, 0, bs_own.at[1], right)
-    b_l1 = b_to(0, 1, 2, 1, bs_own.at[2], left)
     b_l0 = b_to(0, 0, 4, 1, bs_own.at[3], left)
     b_fr = b_to(2, 0, 6, 0, bs_fwd.at[0], right)
     b_fl = b_to(2, 1, 6, 1, bs_fwd.at[1], left)
@@ -131,9 +139,6 @@
 
     def b_wait(u, p):
         b_to(u, p, u, p, bs_rel.at[u, p], mate).wait_recv()
-
-    def lanes_of(xc):
-        return pl.ds(pl.multiple_of(xc * s_chip, s_chip), s_chip)
 
     d_right, d_left, d_opp = 2 * x_r + cc, 2 * x_l + cc, 2 * x_o + cc
     up, lo = pl.ds(0, half), pl.ds(half, half)
@@ -164,6 +169,8 @@
     m_ol.start()
     m_p0.start()
 
+    wblk[...] = jnp.zeros_like(wblk)
+
     for cp in in_small:
         cp.wait()
     def column(row, n, wide):
@@ -174,6 +181,8 @@
     lw = s_loc // 2
     gcol = column(gam[...].astype(F32), n_ch, lw)
     bcol = column(bet[...].astype(F32), n_ch, lw)
+    gb[0] = gcol[:, 0:s_chip]
+    gb[1] = bcol[:, 0:s_chip]
     blc = column(bias_l[...].astype(F32), c_hid, 128)
     brc = column(bias_r[...].astype(F32), c_hid, 128)
     kb = half * n_ch
@@ -224,9 +233,11 @@
         acc = dot(wbig[...], xT[h * kb:(h + 1) * kb, :]) + dot(bbb[h], mk16)
         bT[0, h] = acc.astype(BF16)
         if h == 0:
-            b_r0.start()
+            for k in range(n_f):
+                b_cut(0, k).start()
         else:
-            b_l1.start()
+            for k in range(n_f):
+                b_cut(1, k).start()
             b_l0.start()
             b_r1.start()
         b_rel(0, h).start()
@@ -246,7 +257,6 @@
         at = dot(wa4, xT[g * ka:(g + 1) * ka, :]) + dot(bag, mk16)
         acat[g // 2, :, (g % 2) * 128:(g % 2 + 1) * 128] = at.T.astype(BF16)
 
-    wblk[...] = jnp.zeros_like(wblk)
     lax.fori_loop(0, c_hid // ga, place, 0, unroll=4)
 
     def pair_counts():
@@ -319,6 +329,28 @@
             for k in range(n_d // per):
                 ov[:, chs, k * 128:(k + 1) * 128] = regroup(mr, k, chs, cc)
 
+    def through():
+        for p in range(2):
+            first = (d_right if p else d_left) * n_i + p * half
+            sel = onehot(iota((half, n_j), 1) == iota((half, n_j), 0) + first)
+            mko[p * half:(p + 1) * half, :] = dot_nt(sel, mkl[lanes_of(x_l if p else x_r), :].astype(F32).astype(BF16))
+
+        def norm_via(r, carry):
+            act = tbuf[r // half, r % half].astype(F32)
+            mean = jnp.sum(act, axis=0, keepdims=True) * (1.0 / n_ch)
+            cen = act - mean
+            var = jnp.sum(cen * cen, axis=0, keepdims=True) * (1.0 / n_ch)
+            nrm = cen * lax.rsqrt(var + 1e-5)
+            val = (nrm * gb[0] + gb[1]).astype(BF16) * mko[pl.ds(r, 1), :].astype(BF16)
+            xT[pl.ds(pl.multiple_of(r * n_ch, n_ch), n_ch), 0:s_chip] = val
+            return carry
+
+        lax.fori_loop(0, n_i, norm_via, 0, unroll=4)
+        mko16 = mko[...].astype(BF16)
+        for p in range(2):
+            acc = dot(wbig[...], xT[p * kb:(p + 1) * kb, 0:s_chip]) + dot(bbb[p], mko16)
+            bT[2, p, :, lanes_of(x_l if p else x_r)] = acc.astype(BF16)
+
     def step(t, carry):
         @pl.when(t == 1)
         def _():
@@ -326,26 +358,30 @@
             b_wait(1, 1)
 
         @pl.when(t == 2)
+        def _():
+            m_or.wait_recv()
+            m_ol.wait_recv()
+            through()
+            for k in range(n_f):
+                b_cut(0, k).wait_recv()
+            b_fr.start()
+            b_rel(2, 0).start()
+            for k in range(n_f):
+                b_cut(1, k).wait_recv()
+            b_fl.start()
+            b_rel(2, 1).start()
+            for p in range(n_p):
+                m_dir(0, p).start()
+                m_dir(1, p).start()
+                if p == 1:
+                    m_fr.start()
+                    m_fl.start()
+
+        @pl.when(t == 3)
         def _():
             in_mask.wait()
             in_z.wait()
             pair_counts()
-            b_wait(2, 0)
-            b_fr.start()
-            b_rel(2, 0).start()
-            b_wait(2, 1)
-            b_fl.start()
-            b_rel(2, 1).start()
-            m_or.wait_recv()
-            m_fr.start()
-            m_ol.wait_recv()
-            m_fl.start()
-            for p in range(n_p):
-                m_dir(0, p).start()
-                m_dir(1, p).start()
-
-        @pl.when(t == 3)
-        def _():
             b_wait(3, 0)
             b_wait(3, 1)
 
@@ -393,35 +429,36 @@
                 lax.fori_loop(0, half, add, 0, unroll=4)
                 y2(v, f).start()
 
-        @pl.when(t == 6 + LAG2)
+        @pl.when(t == 8)
         def _():
             m_self.wait()
+            m_land(0)
+            m_land(1)
             for k in range(2):
                 m_fr.wait_recv() if k == 0 else m_fl.wait_recv()
                 m_p3[k].start()
-            m_land(0)
             m_p0.wait_recv()
             for k in range(2):
                 m_p3[k].wait_recv()
-            m_land(1)
             m_part(0)
+            m_part(1)
 
         @pl.when(t >= LAG2)
         def _():
             finish(t - LAG2)
 
-        @pl.when(t == 7 + LAG2)
-        def _():
-            for p in range(2, n_p):
-                m_land(p)
-                m_part(p - 1)
-            m_part(n_p - 1)
+        @pl.when(t == 9)
+        def _():
+            m_land(2)
+            m_land(3)
+            m_part(2)
+            m_part(3)
 
         return carry
 
     lax.fori_loop(0, 8 + LAG2, step, 0)
 
-    for cp in (b_r0, b_r1, b_l1, b_l0, b_fr, b_fl, m_or, m_ol, m_fr, m_fl, m_p0, *m_p3):
+    for cp in (*(b_cut(p, k) for p in range(2) for k in range(n_f)), b_r1, b_l0, b_fr, b_fl, m_or, m_ol, m_fr, m_fl, m_p0, *m_p3):
         cp.wait_send()
     for k in range(2):
         for p in range(n_p):
@@ -484,7 +521,9 @@
                 pltpu.VMEM(ysh, BF16),
                 pltpu.VMEM((n_j, 128), F32),
                 pltpu.VMEM((2, half, n_ch, s_loc * 2 // n_d), BF16),
-                dma((5,)), dma((8,)), dma((4,)), dma((2,)), dma((8, 2)), dma((8, 2)),
+                pltpu.VMEM((2, n_ch, s_loc * 2 // n_d), F32),
+                pltpu.VMEM((n_i, s_loc * 2 // n_d), F32),
+                dma((5,)), dma((8,)), dma((4,)), dma((2,)), dma((8, 2)), dma((8, 2)), dma((2, 4)), dma((2, 4)),
                 dma((2, 4)), dma((2,)), dma((2,)), dma((3, 4)), dma((2, 4)), dma((2,)), dma((2,)), dma((3, 4)),
                 dma((8, 2)), dma((8, 2)), dma((8, 2)), dma((8, 2)),
             ],

time: 74 us -> 71.2 us (0.962)
  Pallas kernels: 73.2 us -> 70.4 us
    pallas_call x1, Pallas kernels: 70.5 us -> 67.7 us  [local_fn(): pl.pallas_call(functools.partial(kernel, (n_y, n_d)), out_shape=(pltpu.VM...]
where the time goes in v4:
time: 71.2 us; the launch traced here: 71.1 us
  Pallas kernels  70.4 us (99%)
    pallas_call x1, Pallas kernels, local_fn(): pl.pallas_call(functools.partial(kernel, (n_y, n_d)), out_shape=(pltpu.VM...  67.7 us
    pallas_call x1, Pallas kernels, local_fn(): pl.pallas_call(put_out, out_shape=(jax.ShapeDtypeStruct(z.shape, F32), ja...  2.7 us

profile of v4, /device:TPU:97, one launch (start us, length us, event | category | flops | bytes accessed | tf_op | source)
XLA Modules:
  0.0 71.1 jit_solution(15028282327759318226)
XLA Ops:
  0.6 67.7 %opm.1 = (f32[32,256,128]{2,1,0:T(8,128)S(1)}, bf16[64,64,256]{2,1,0:T(8,128)(2,1)S(1)}, bf16[8,32,64,128]{3,2,1,0:T(8,128)(2,1)S(1)}) custom-call(bf16[32,64,512]{2,1,0:T(8,128)(2,1)} %bitcast.9, s32[2048,256]{1,0:T(8,128)} %mask_hbm.1, f32[32,256,128]{2,1,0:T(8,128)} %z_hbm.1, bf16[1,64]{1,0:T(2,128)(2,1)} %bitcast.12, bf16[1,64]{1,0:T(2,128)(2,1)} %bitcast.13, ...), custom_call_target="tpu_custom_call" | custom-call | tf_op jit(solution)/shard_map/opm/pallas_call | solution.py:501
  68.4 2.7 %out.1 = (f32[32,256,128]{2,1,0:T(8,128)}, bf16[64,64,256]{2,1,0:T(8,128)(2,1)}) custom-call(f32[32,256,128]{2,1,0:T(8,128)S(1)} %get-tuple-element.7.z_ref, bf16[64,64,256]{2,1,0:T(8,128)(2,1)S(1)} %get-tuple-element.8.o_ref, bf16[8,32,64,128]{3,2,1,0:T(8,128)(2,1)S(1)} %get-tuple-element.9.mr), custom_call_target="tpu_custom_call" | custom-call | tf_op jit(solution)/shard_map/out/pallas_call | solution.py:533

commit v5 on v4

--- a/solution.py
+++ b/solution.py
@@ -44,16 +44,16 @@
 
 def put_out(z_ref, o_ref, mr, zo_hbm, mo_hbm, last, sem):
     cc = lax.axis_index("dap") % 2
-    n_z = z_ref.shape[0] // 4
+    n_z = z_ref.shape[0] // 8
     n_ch = o_ref.shape[1]
     ch_p = last.shape[1]
-    outs = [pltpu.make_async_copy(z_ref.at[k * n_z:(k + 1) * n_z], zo_hbm.at[k * n_z:(k + 1) * n_z], sem.at[k]) for k in range(4)]
-    outs.append(pltpu.make_async_copy(o_ref.at[:, 0:n_ch - ch_p], mo_hbm.at[:, 0:n_ch - ch_p], sem.at[4]))
+    outs = [pltpu.make_async_copy(z_ref.at[k * n_z:(k + 1) * n_z], zo_hbm.at[k * n_z:(k + 1) * n_z], sem.at[k]) for k in range(8)]
+    outs.append(pltpu.make_async_copy(o_ref.at[:, 0:n_ch - ch_p], mo_hbm.at[:, 0:n_ch - ch_p], sem.at[8]))
     for o in outs:
         o.start()
     for k in range(last.shape[2] // 128):
         last[:, :, k * 128:(k + 1) * 128] = regroup(mr, k, pl.ds(n_ch - ch_p, ch_p), cc)
-    tail = pltpu.make_async_copy(last, mo_hbm.at[:, n_ch - ch_p:], sem.at[5])
+    tail = pltpu.make_async_copy(last, mo_hbm.at[:, n_ch - ch_p:], sem.at[9])
     tail.start()
     for o in outs + [tail]:
         o.wait()
@@ -379,14 +379,14 @@
 
         @pl.when(t == 3)
         def _():
+            b_wait(3, 0)
+            b_wait(3, 1)
+
+        @pl.when(t == 4)
+        def _():
             in_mask.wait()
             in_z.wait()
             pair_counts()
-            b_wait(3, 0)
-            b_wait(3, 1)
-
-        @pl.when(t == 4)
-        def _():
             b_wait(4, 0)
             b_rel(4, 0).start()
             b_wait(4, 1)
@@ -443,7 +443,11 @@
             m_part(0)
             m_part(1)
 
-        @pl.when(t >= LAG2)
+        @pl.when(t == 4)
+        def _():
+            finish(0)
+
+        @pl.when(t >= 4)
         def _():
             finish(t - LAG2)
 
@@ -535,7 +539,7 @@
             out_shape=(jax.ShapeDtypeStruct(z.shape, F32), jax.ShapeDtypeStruct((s_dev, n_ch, n_j), BF16)),
             in_specs=[vm] * 3,
             out_specs=(any_spec, any_spec),
-            scratch_shapes=[pltpu.VMEM((s_dev, n_ch // 4, n_j), BF16), dma((6,))],
+            scratch_shapes=[pltpu.VMEM((s_dev, n_ch // 4, n_j), BF16), dma((10,))],
             compiler_params=pltpu.CompilerParams(vmem_limit_bytes=10 * 2**20),
             name="out",
         )(*held)

time: 71.2 us -> 71.2 us (level)
  no operation moved by 1% of the time
where the time goes in v5:
time: 71.2 us; the launch traced here: 71.1 us
  Pallas kernels  70.5 us (99%)
    pallas_call x1, Pallas kernels, local_fn(): pl.pallas_call(functools.partial(kernel, (n_y, n_d)), out_shape=(pltpu.VM...  67.7 us
    pallas_call x1, Pallas kernels, local_fn(): pl.pallas_call(put_out, out_shape=(jax.ShapeDtypeStruct(z.shape, F32), ja...  2.73 us

profile of v5, /device:TPU:97, one launch (start us, length us, event | category | flops | bytes accessed | tf_op | source)
XLA Modules:
  0.0 71.1 jit_solution(14613610236206052100)
XLA Ops:
  0.6 67.7 %opm.1 = (f32[32,256,128]{2,1,0:T(8,128)S(1)}, bf16[64,64,256]{2,1,0:T(8,128)(2,1)S(1)}, bf16[8,32,64,128]{3,2,1,0:T(8,128)(2,1)S(1)}) custom-call(bf16[32,64,512]{2,1,0:T(8,128)(2,1)} %bitcast.9, s32[2048,256]{1,0:T(8,128)} %mask_hbm.1, f32[32,256,128]{2,1,0:T(8,128)} %z_hbm.1, bf16[1,64]{1,0:T(2,128)(2,1)} %bitcast.12, bf16[1,64]{1,0:T(2,128)(2,1)} %bitcast.13, ...), custom_call_target="tpu_custom_call" | custom-call | tf_op jit(solution)/shard_map/opm/pallas_call | solution.py:505
  68.4 2.7 %out.1 = (f32[32,256,128]{2,1,0:T(8,128)}, bf16[64,64,256]{2,1,0:T(8,128)(2,1)}) custom-call(f32[32,256,128]{2,1,0:T(8,128)S(1)} %get-tuple-element.7.z_ref, bf16[64,64,256]{2,1,0:T(8,128)(2,1)S(1)} %get-tuple-element.8.o_ref, bf16[8,32,64,128]{3,2,1,0:T(8,128)(2,1)S(1)} %get-tuple-element.9.mr), custom_call_target="tpu_custom_call" | custom-call | tf_op jit(solution)/shard_map/out/pallas_call | solution.py:537
